TPU v7x, 256 devices: a whole 4x4x8 slice. The times are simulated.
256 devices in a mesh: row: 32 (over y, x, core), col: 8 (over z).
Axes of the slice: x: 4, y: 4, z: 8, core: 2. Of those that a mesh axis runs over, the one named last changes fastest.
Arguments:
- covariance: bfloat16 [16384, 16384], P('row', 'col'), may hold values from -0.12 to 0.6, as said below
- estimate: bfloat16 [16384, 16384], P('row', 'col'), may hold values from -2.3 to 12, as said below
- dual_var: bfloat16 [16384, 16384], P('row', 'col'), may hold values from -1.7 to 1.7, as said below
- start_basis: float32 [16384, 128], P('row'), may hold values from -6 to 6
Outputs:
- next_estimate: float32 [16384, 16384], P('row', 'col')
- next_dual: bfloat16 [16384, 16384], P('row', 'col')
Inputs may be any that keep to these rules, and one draw needn't show every extreme that they name: `covariance`: symmetric. `estimate`: symmetric. `dual_var`: symmetric.
All inputs are finite; a program needn't handle non-finite values.
Results may differ from a plain program's by a relative error of at most 0.001.
Values sent between devices are 32-bit elements; how exact they have to be, the bound alone decides.
A program may use at most 64 MiB of HBM per device.

v0:
```python
import jax
import jax.numpy as jnp
from jax import lax
from jax.sharding import PartitionSpec as P

NS_ITERS = 12


penalty = 0.01
threshold = 0.2
base_level = 10.0
highest = lax.Precision.HIGHEST


def sent_to_all(array, axis):
    copies = jnp.broadcast_to(array, (lax.axis_size(axis), *array.shape))
    return lax.all_to_all(copies, axis, split_axis=0, concat_axis=0, tiled=True)


def taken_together(array, axis):
    everything = sent_to_all(array, axis)
    return jnp.sum(everything, axis=0)


def picked(array, axis, root):
    return lax.dynamic_index_in_dim(lax.all_gather(array, axis), root, 0, keepdims=False)


def inner_product(left_side, right_side):
    return lax.dot_general(
        left_side,
        right_side,
        (((0,), (0,)), ((), ())),
        precision=highest,
        preferred_element_type=jnp.float32,
    )


def normalize(mapped, gram_matrix):
    lower_factor = jnp.linalg.cholesky(gram_matrix)
    identity = jnp.eye(gram_matrix.shape[0], dtype=jnp.float32)
    inverse = lax.linalg.triangular_solve(lower_factor, identity, left_side=True, lower=True)
    return jnp.dot(mapped, inverse.T, precision=highest, preferred_element_type=jnp.float32)


def response_of(ritz_matrix):
    identity = jnp.eye(ritz_matrix.shape[0], dtype=jnp.float32)
    square = (
        jnp.dot(ritz_matrix, ritz_matrix, precision=highest, preferred_element_type=jnp.float32)
        + 4.0 * penalty * identity
    )
    frobenius = jnp.sqrt(jnp.sum(square * square))

    def newton(sweep_index, state_pair):
        iterate, partner = state_pair
        factor = 0.5 * (
            3.0 * identity
            - jnp.dot(partner, iterate, precision=highest, preferred_element_type=jnp.float32)
        )
        return (
            jnp.dot(iterate, factor, precision=highest, preferred_element_type=jnp.float32),
            jnp.dot(factor, partner, precision=highest, preferred_element_type=jnp.float32),
        )

    iterate, partner = lax.fori_loop(0, NS_ITERS, newton, (square / frobenius, identity))
    square_root = jnp.sqrt(frobenius) * iterate
    return (ritz_matrix + square_root) / (2.0 * penalty) - base_level * identity


def column_basis(shifted, row_basis):
    partial_terms = lax.dot_general(
        shifted,
        row_basis,
        (((0,), (0,)), ((), ())),
        precision=highest,
        preferred_element_type=jnp.float32,
    )
    mapped = lax.psum(partial_terms, "row")
    gram_matrix = taken_together(inner_product(mapped, mapped), "col")
    return normalize(mapped, gram_matrix)


def row_image(shifted, col_basis):
    local_terms = jnp.dot(shifted, col_basis, precision=highest, preferred_element_type=jnp.float32)
    return taken_together(local_terms, "col")


def row_inner(left_side, right_side):
    return taken_together(inner_product(left_side, right_side), "row")


def body(covariance, estimate, dual_var, start_basis):
    shifted = penalty * (
        estimate.astype(jnp.float32) - dual_var.astype(jnp.float32)
    ) - covariance.astype(jnp.float32)
    rows_tile = shifted.shape[0]
    cols_tile = shifted.shape[1]
    row_basis = start_basis
    col_basis = column_basis(shifted, row_basis)
    blocks_per_column = lax.axis_size("row") // lax.axis_size("col")
    row_index = lax.axis_index("row")
    own_block = lax.dynamic_slice_in_dim(
        col_basis, row_index % blocks_per_column * rows_tile, rows_tile, 0
    )
    row_basis = picked(own_block, "col", row_index // blocks_per_column)
    product = row_image(shifted, col_basis)
    raw_ritz = row_inner(row_basis, product)
    ritz_matrix = 0.5 * (raw_ritz + raw_ritz.T)
    response = response_of(ritz_matrix)
    weighted = jnp.dot(row_basis, response, precision=highest, preferred_element_type=jnp.float32)
    theta_tile = lax.dot_general(
        weighted,
        col_basis,
        (((1,), (1,)), ((), ())),
        precision=highest,
        preferred_element_type=jnp.float32,
    )
    row_ids = row_index * rows_tile + lax.broadcasted_iota(jnp.int32, (rows_tile, 1), 0)
    col_ids = lax.axis_index("col") * cols_tile + lax.broadcasted_iota(jnp.int32, (1, cols_tile), 1)
    theta_tile = theta_tile + jnp.where(row_ids == col_ids, base_level, 0.0)
    mixture = theta_tile + dual_var.astype(jnp.float32)
    clipped = jnp.clip(mixture, -threshold, threshold)
    return (mixture - clipped, clipped.astype(jnp.bfloat16))


def solution(mesh):
    return jax.shard_map(
        body,
        mesh=mesh,
        in_specs=(P("row", "col"), P("row", "col"), P("row", "col"), P("row", None)),
        out_specs=(P("row", "col"), P("row", "col")),
        check_vma=False,
    )
```

profile of v0, /device:TPU:1, one launch (start us, length us, event | category | flops | bytes accessed | tf_op | source)
XLA Modules:
  0.0 345.5 jit_solution(5025053525207511477)
XLA Ops:
  7.2 0.9 copy-done
  8.1 10.0 %fusion.7 = f32[2048,128]{1,0:T(8,128)} fusion(f32[512,128]{1,0:T(8,128)S(1)} %copy-done, bf16[512,2048]{1,0:T(8,128)(2,1)} %param.8, bf16[512,2048]{1,0:T(8,128)(2,1)} %param.6, bf16[512,2048]{1,0:T(8,128)(2,1)} %param.7), kind=kOutput, calls=%fused_computation.12 | convolution fusion | flops 1616904192 | bytes 7602176 | tf_op jit(solution)/shard_map/dot_general | solution.py:71
  18.1 119.4 %all-reduce.2.cloned.1.call-done = f32[2048,128]{1,0:T(8,128)} async-done(((f32[2048,128]{1,0:T(8,128)}), f32[2048,128]{1,0:T(8,128)}) %all-reduce.2.cloned.1.call-update) | async-done | bytes 1048592 | tf_op jit(solution)/shard_map/psum | solution.py:78
  137.5 3.4 fusion.44
  140.8 0.8 broadcast_in_dim.19
  141.7 6.7 %all-to-all-start = ((f32[8,128,128]{2,1,0:T(8,128)}), f32[8,128,128]{2,1,0:T(8,128)S(1)}, u32[]{:S(2)}, u32[]{:S(2)}) async-start(f32[8,128,128]{2,1,0:T(8,128)} %broadcast_in_dim.19), calls=%async_computation | async-start | bytes 1048576 | tf_op jit(solution)/shard_map/all_to_all | solution.py:17
  148.4 18.0 %all-to-all-done = f32[8,128,128]{2,1,0:T(8,128)S(1)} async-done(((f32[8,128,128]{2,1,0:T(8,128)}), f32[8,128,128]{2,1,0:T(8,128)S(1)}, u32[]{:S(2)}, u32[]{:S(2)}) %all-to-all-start) | async-done | bytes 524320 | tf_op jit(solution)/shard_map/all_to_all | solution.py:17
  166.5 11.7 %cholesky.21 = f32[128,128]{1,0:T(8,128)S(1)} custom-call(f32[128,128]{1,0:T(8,128)S(1)} %fusion.21), custom_call_target="Cholesky" | custom-call | tf_op jit(solution)/shard_map/jit(cholesky)/cholesky | solution.py:40
  178.2 0.6 compare_reduce_fusion
  178.9 0.7 fusion.17
  179.6 9.8 %custom-call.6 = f32[1,128,128]{1,2,0:T(8,128)S(1)} custom-call(f32[1,128,128]{2,1,0:T(8,128)S(1)} %fusion.17), custom_call_target="InvertDiagBlocksLowerTriangular" | custom-call | tf_op jit(solution)/shard_map/triangular_solve | solution.py:42
  189.4 0.2 fusion.19
  189.6 2.2 fusion.45
  191.8 6.2 %fusion.5 = f32[512,128]{1,0:T(8,128)S(1)} fusion(f32[2048,128]{1,0:T(8,128)S(1)} %fusion.45, bf16[512,2048]{1,0:T(8,128)(2,1)S(1)} %copy-done.1, bf16[512,2048]{1,0:T(8,128)(2,1)} %param.6, bf16[512,2048]{1,0:T(8,128)(2,1)} %param.7), kind=kOutput, calls=%fused_computation.11 | convolution fusion | flops 1616904192 | bytes 7602176 | tf_op jit(solution)/shard_map/dot_general | solution.py:84
  198.0 1.5 broadcast_in_dim.20
  199.5 4.4 %all-to-all-start.1 = ((f32[8,512,128]{2,1,0:T(8,128)}), f32[8,512,128]{2,1,0:T(8,128)}, u32[]{:S(2)}, u32[]{:S(2)}) async-start(f32[8,512,128]{2,1,0:T(8,128)} %broadcast_in_dim.20), calls=%async_computation.1 | async-start | bytes 4194304 | tf_op jit(solution)/shard_map/all_to_all | solution.py:17
  203.9 0.3 all-gather.3.cloned.1.call-start
  204.1 0.7 constant_dynamic-slice_fusion
  204.9 64.8 %all-to-all-done.1 = f32[8,512,128]{2,1,0:T(8,128)} async-done(((f32[8,512,128]{2,1,0:T(8,128)}), f32[8,512,128]{2,1,0:T(8,128)}, u32[]{:S(2)}, u32[]{:S(2)}) %all-to-all-start.1) | async-done | bytes 2097184 | tf_op jit(solution)/shard_map/all_to_all | solution.py:17
  269.7 2.4 reduce_sum.37
  272.2 1.4 all-gather.3.cloned.1.call-done
  273.5 1.6 fusion.13
  275.2 1.6 broadcast_in_dim.21
  276.7 6.7 %all-to-all-start.2 = ((f32[32,128,128]{2,1,0:T(8,128)}), f32[32,128,128]{2,1,0:T(8,128)}, u32[]{:S(2)}, u32[]{:S(2)}) async-start(f32[32,128,128]{2,1,0:T(8,128)} %broadcast_in_dim.21), calls=%async_computation.2 | async-start | bytes 4194304 | tf_op jit(solution)/shard_map/all_to_all | solution.py:17
  283.5 28.7 %all-to-all-done.2 = f32[32,128,128]{2,1,0:T(8,128)} async-done(((f32[32,128,128]{2,1,0:T(8,128)}), f32[32,128,128]{2,1,0:T(8,128)}, u32[]{:S(2)}, u32[]{:S(2)}) %all-to-all-start.2) | async-done | bytes 2097184 | tf_op jit(solution)/shard_map/all_to_all | solution.py:17
  312.1 1.7 reduce_sum.38
  313.9 0.7 copy.11
  314.6 2.4 multiply_reduce_fusion
  317.7 1.5 broadcast_divide_fusion
  319.2 0.9 copy.12
  320.1 9.8 %while.13 = (s32[]{:T(128)}, f32[128,128]{0,1:T(8,128)S(1)}, f32[128,128]{1,0:T(8,128)S(1)}, s32[]{:T(128)}) while((s32[]{:T(128)}, f32[128,128]{0,1:T(8,128)S(1)}, f32[128,128]{1,0:T(8,128)S(1)}, s32[]{:T(128)}) %tuple.30), condition=%wide.region_8.9_spmd.clone, body=%wide.region_7.8_spmd.clone.sunk | while | flops 75563008 | bytes 852021 | solution.py:65
  320.2 0.3 fusion.75
  320.4 0.2 fusion.76
  320.7 0.3 convolution_bitcast_fusion.2
  321.0 0.3 fusion.75
  321.3 0.2 fusion.76
  321.5 0.3 convolution_bitcast_fusion.2
  321.8 0.3 fusion.75
  322.3 0.3 convolution_bitcast_fusion.2
  322.6 0.3 fusion.75
  323.1 0.3 convolution_bitcast_fusion.2
  323.4 0.3 fusion.75
  323.7 0.2 fusion.76
  323.9 0.3 convolution_bitcast_fusion.2
  324.3 0.3 fusion.75
  324.5 0.2 fusion.76
  324.7 0.3 convolution_bitcast_fusion.2
  325.1 0.3 fusion.75
  325.3 0.2 fusion.76
  325.6 0.3 convolution_bitcast_fusion.2
  325.9 0.3 fusion.75
  326.2 0.2 fusion.76
  326.4 0.3 convolution_bitcast_fusion.2
  326.7 0.3 fusion.75
  327.2 0.3 convolution_bitcast_fusion.2
  327.5 0.3 fusion.75
  328.0 0.3 convolution_bitcast_fusion.2
  328.3 0.3 fusion.75
  328.8 0.3 convolution_bitcast_fusion.2
  329.2 0.3 fusion.75
  329.6 0.3 convolution_bitcast_fusion.2
  330.0 1.4 fusion.11
  331.4 5.8 %clamp_subtract_fusion = (f32[512,2048]{1,0:T(8,128)}, bf16[512,2048]{1,0:T(8,128)(2,1)S(1)}) fusion(bf16[512,2048]{1,0:T(8,128)(2,1)S(1)} %copy-done.1, s32[2048]{0:T(1024)S(1)} %iota_add_fusion, s32[512]{0:T(512)S(1)} %iota_add_fusion.1, f32[512,128]{1,0:T(8,128)S(1)} %fusion.11, f32[2048,128]{1,0:T(8,128)S(1)} %fusion.45), kind=kOutput, calls=%fused_computation.6 | convolution fusion | flops 1619001344 | bytes 9709568 | tf_op jit(solution)/shard_map/dot_general | solution.py:111
  337.2 1.5 clamp_convert_fusion
  (46 shorter events, 1.7 us)
Async XLA Ops:
  7.2 1.0 copy-start
  7.2 130.3 %all-reduce.2.cloned.1.call-start = ((), (), s32[]{:S(2)}) async-start(), calls=%async_computation.3 | async-start | bytes 2097152 | tf_op jit(solution)/shard_map/psum | solution.py:78
  18.1 173.8 %copy-start.1 = (bf16[512,2048]{1,0:T(8,128)(2,1)S(1)}, bf16[512,2048]{1,0:T(8,128)(2,1)}, u32[]{:S(2)}) copy-start(bf16[512,2048]{1,0:T(8,128)(2,1)} %param.8) | copy-start | bytes 6291460
  141.7 24.7 %all-to-all-start = ((f32[8,128,128]{2,1,0:T(8,128)}), f32[8,128,128]{2,1,0:T(8,128)S(1)}, u32[]{:S(2)}, u32[]{:S(2)}) async-start(f32[8,128,128]{2,1,0:T(8,128)} %broadcast_in_dim.19), calls=%async_computation | async-start | bytes 1048576 | tf_op jit(solution)/shard_map/all_to_all | solution.py:17
  199.5 70.3 %all-to-all-start.1 = ((f32[8,512,128]{2,1,0:T(8,128)}), f32[8,512,128]{2,1,0:T(8,128)}, u32[]{:S(2)}, u32[]{:S(2)}) async-start(f32[8,512,128]{2,1,0:T(8,128)} %broadcast_in_dim.20), calls=%async_computation.1 | async-start | bytes 4194304 | tf_op jit(solution)/shard_map/all_to_all | solution.py:17
  203.9 69.7 %all-gather.3.cloned.1.call-start = ((), (), s32[]{:S(2)}) async-start(), calls=%async_computation.4 | async-start | bytes 2359296 | tf_op jit(solution)/shard_map/all_gather | solution.py:26
  276.7 35.4 %all-to-all-start.2 = ((f32[32,128,128]{2,1,0:T(8,128)}), f32[32,128,128]{2,1,0:T(8,128)}, u32[]{:S(2)}, u32[]{:S(2)}) async-start(f32[32,128,128]{2,1,0:T(8,128)} %broadcast_in_dim.21), calls=%async_computation.2 | async-start | bytes 4194304 | tf_op jit(solution)/shard_map/all_to_all | solution.py:17
  313.8 3.9 %copy-start.2 = (f32[128,128]{1,0:T(8,128)}, f32[128,128]{1,0:T(8,128)S(1)}, u32[]{:S(2)}) copy-start(f32[128,128]{1,0:T(8,128)S(1)} %reduce_sum.38) | copy-start | bytes 196612
Sparse Core Ops, SparseCore 0:
  18.2 119.2 all-reduce.1
  207.0 66.4 all-gather.2
where the time goes:
time: 347 us; the launch traced here: 346 us
  waiting for transfers between devices  232 us (67%)
  matrix products  42.2 us (12%)
  other arithmetic  30 us (9%)
  starting transfers between devices  18.1 us (5%)
  between operations  14.9 us (4%)
  local copies, waits for them, and re-layouts  7.46 us (2%)
    psum x1, waiting for transfers between devices, column_basis(): mapped = lax.psum(partial_terms, 'row')  119 us
    all_to_all x3, waiting for transfers between devices, sent_to_all(): return lax.all_to_all(copies, axis, split_axis=0, concat_axis=0, tiled=True)  111 us
    all_to_all x3, starting transfers between devices, sent_to_all(): return lax.all_to_all(copies, axis, split_axis=0, concat_axis=0, tiled=True)  17.8 us
    another operation x3, other arithmetic, normalize(): lower_factor = jnp.linalg.cholesky(gram_matrix)  12.4 us
    another operation x2, other arithmetic, normalize(): lax.linalg.triangular_solve(lower_factor, identity, left_side=True, lower...  10.5 us
    dot_general x1, matrix products, column_basis(): lax.dot_general(shifted, row_basis, (((0,), (0,)), ((), ())), precision=h...  9.96 us
  transfers between devices with their start and end apart: 5, of which 5 were waited for; matrix products, arithmetic and copies ran while one was open for 1% of the time, Pallas kernels for 0%

commit v1 on v0

v1 whole, which is shorter than its diff:
```python
import functools

import jax
import jax.numpy as jnp
from jax import lax
from jax.experimental import pallas as pl
from jax.experimental.pallas import tpu as pltpu
from jax.sharding import PartitionSpec as P

NS_ITERS = 12
MESH = pl.DeviceIdType.MESH
F32 = jnp.float32
BF16 = jnp.bfloat16

penalty = 0.01
threshold = 0.2
base_level = 10.0
highest = lax.Precision.HIGHEST

NN = (((1,), (0,)), ((), ()))
NT = (((1,), (1,)), ((), ()))
TN = (((0,), (0,)), ((), ()))

PLANE = 16
DEPTH = 8
CHUNK = 64


def dot(left, right, dims=NN):
    return lax.dot_general(left, right, dims, preferred_element_type=F32)


def dot_full(left, right, dims=NN):
    return lax.dot_general(left, right, dims, precision=highest, preferred_element_type=F32)


def split(array):
    high = array.astype(BF16)
    return high, (array - high.astype(F32)).astype(BF16)


def dot_split(left, right, dims=NN):
    left_high, left_low = split(left)
    right_high, right_low = split(right)
    return dot(left_high, right_high, dims) + (
        dot(left_low, right_high, dims) + dot(left_high, right_low, dims)
    )


def loop(low, high, body):
    def step(index, carry):
        body(index)
        return carry

    lax.fori_loop(low, high, step, 0)


def solve_kernel(
    cov_hbm,
    est_hbm,
    dual_hbm,
    basis,
    left_out,
    right_out,
    cov,
    est,
    dual,
    a_high,
    a_low,
    part_other,
    part_own,
    half_in,
    rs_send,
    rs_in,
    image,
    z_in,
    rows_in,
    product,
    red_part,
    red_in,
    red_mid,
    red_mid_in,
    red_out,
    table,
    pair,
    load_sem,
    half_send,
    half_recv,
    rs_ssem,
    rs_rsem,
    ag_ssem,
    ag_rsem,
    fwd_send,
    fwd_recv,
    z_ssem,
    z_rsem,
    rows_ssem,
    rows_rsem,
    a_ssem,
    a_rsem,
    b_ssem,
    b_rsem,
    c_ssem,
    c_rsem,
):
    row = lax.axis_index("row")
    col = lax.axis_index("col")
    core = lax.rem(row, 2)
    chip = lax.div(row, 2)
    other = row + 1 - 2 * core
    own_chunk = core * PLANE + chip

    half = a_high.shape[1] // 2

    def load(index, side):
        source, target = ((cov_hbm, cov), (est_hbm, est), (dual_hbm, dual))[index]
        offset = pl.multiple_of((1 - core if side == 0 else core) * half, half)
        window = pl.ds(offset, half)
        return pltpu.make_async_copy(
            source.at[:, window], target.at[:, window], load_sem.at[index, side]
        )

    for side in range(2):
        for index in range(3):
            load(index, side).start()

    def plane_row(offset):
        return 2 * lax.rem(chip + offset, PLANE) + core

    def column_device(offset):
        target = lax.rem(2 * col + core + offset, 2 * DEPTH)
        return (2 * chip + lax.rem(target, 2), lax.div(target, 2))

    def rows_source(index):
        chunk = 8 * lax.rem(row, 4) + index
        return 2 * lax.rem(chunk, PLANE) + lax.div(chunk, PLANE)

    def rows_target(index):
        return 4 * index + lax.div(own_chunk, 8)

    barrier = pltpu.get_barrier_semaphore()

    def signal(device):
        pl.semaphore_signal(barrier, inc=1, device_id=device, device_id_type=MESH)

    loop(1, PLANE, lambda d: signal((plane_row(d), col)))
    loop(1, 2 * DEPTH, lambda d: signal(column_device(d)))

    def signal_source(index):
        source = rows_source(index)

        @pl.when(source != row)
        def _():
            signal((source, col))

    loop(0, 8, signal_source)

    has_own = lax.rem(row, 4) == lax.div(own_chunk, 8)
    peers = PLANE - 1 + 2 * DEPTH - 1 + 8 - jnp.where(has_own, 1, 0)

    flipped = basis[...].T
    flip_high, flip_low = split(flipped)
    flip_both = jnp.concatenate([flip_high, flip_low], axis=0)
    width = 256
    rank = flipped.shape[0]

    def partial_terms(side, target):
        offset = (1 - core if side == 0 else core) * half

        def block(index):
            window = pl.ds(pl.multiple_of(offset + index * width, width), width)
            shifted = penalty * (
                est[:, window].astype(F32) - dual[:, window].astype(F32)
            ) - cov[:, window].astype(F32)
            high, low = split(shifted)
            a_high[:, window] = high
            a_low[:, window] = low
            both = dot(flip_both, high)
            terms = both[:rank] + both[rank:] + dot(flip_high, low)
            pieces = width // CHUNK
            target[pl.ds(pieces * index, pieces)] = terms.T.reshape(pieces, CHUNK, rank)

        loop(0, half // width, block)

    for index in range(3):
        load(index, 0).wait()
    partial_terms(0, part_other)

    pl.semaphore_wait(barrier, peers)

    half_copy = pltpu.make_async_remote_copy(
        src_ref=part_other,
        dst_ref=half_in,
        send_sem=half_send,
        recv_sem=half_recv,
        device_id=(other, col),
        device_id_type=MESH,
    )
    half_copy.start()
    for index in range(3):
        load(index, 1).wait()
    partial_terms(1, part_own)
    half_copy.wait_recv()
    rs_send[...] = part_own[...] + half_in[...]

    def rs_copy(d):
        return pltpu.make_async_remote_copy(
            src_ref=rs_send.at[lax.rem(chip + d, PLANE)],
            dst_ref=rs_in.at[d],
            send_sem=rs_ssem.at[d],
            recv_sem=rs_rsem.at[d],
            device_id=(plane_row(d), col),
            device_id_type=MESH,
        )

    loop(1, PLANE, lambda d: rs_copy(d).start())
    total = rs_send[chip]
    loop(1, PLANE, lambda d: rs_copy(d).wait_recv())
    for d in range(1, PLANE):
        total = total + rs_in[d]
    image[own_chunk] = total
    z_in[col] = total

    def z_copy(d):
        return pltpu.make_async_remote_copy(
            src_ref=image.at[own_chunk],
            dst_ref=z_in.at[col],
            send_sem=z_ssem.at[d],
            recv_sem=z_rsem.at[d],
            device_id=(row, lax.rem(col + d, DEPTH)),
            device_id_type=MESH,
        )

    def ag_copy(d):
        return pltpu.make_async_remote_copy(
            src_ref=image.at[own_chunk],
            dst_ref=image.at[own_chunk],
            send_sem=ag_ssem.at[d],
            recv_sem=ag_rsem.at[d],
            device_id=(plane_row(d), col),
            device_id_type=MESH,
        )

    loop(1, DEPTH, lambda d: z_copy(d).start())
    loop(1, PLANE, lambda d: ag_copy(d).start())

    def a_copy(which, d):
        return pltpu.make_async_remote_copy(
            src_ref=red_part.at[which, lax.rem(chip + d, PLANE)],
            dst_ref=red_in.at[which, d],
            send_sem=a_ssem.at[which, d],
            recv_sem=a_rsem.at[which, d],
            device_id=(plane_row(d), col),
            device_id_type=MESH,
        )

    def b_copy(which, d):
        return pltpu.make_async_remote_copy(
            src_ref=red_mid.at[which],
            dst_ref=red_mid_in.at[which, d],
            send_sem=b_ssem.at[which, d],
            recv_sem=b_rsem.at[which, d],
            device_id=column_device(d),
            device_id_type=MESH,
        )

    def c_copy(which, d):
        return pltpu.make_async_remote_copy(
            src_ref=red_out.at[which, chip],
            dst_ref=red_out.at[which, chip],
            send_sem=c_ssem.at[which, d],
            recv_sem=c_rsem.at[which, d],
            device_id=(plane_row(d), col),
            device_id_type=MESH,
        )

    def reduce_start(which, value):
        red_part[which] = value.reshape(PLANE, 8, rank)
        loop(1, PLANE, lambda d: a_copy(which, d).start())

    def reduce_middle(which):
        loop(1, PLANE, lambda d: a_copy(which, d).wait_recv())
        piece = red_part[which, chip]
        for d in range(1, PLANE):
            piece = piece + red_in[which, d]
        red_mid[which] = piece
        loop(1, 2 * DEPTH, lambda d: b_copy(which, d).start())

    def reduce_spread(which):
        loop(1, 2 * DEPTH, lambda d: b_copy(which, d).wait_recv())
        piece = red_mid[which]
        for d in range(1, 2 * DEPTH):
            piece = piece + red_mid_in[which, d]
        red_out[which, chip] = piece
        loop(1, PLANE, lambda d: c_copy(which, d).start())

    def reduce_end(which):
        loop(1, PLANE, lambda d: c_copy(which, d).wait_recv())
        return red_out[which].reshape(rank, rank)

    reduce_start(0, dot_full(total, total, TN))

    loop(1, DEPTH, lambda d: z_copy(d).wait_recv())
    slot = lax.rem(own_chunk, 8)

    def rows_copy(index):
        return pltpu.make_async_remote_copy(
            src_ref=z_in.at[index],
            dst_ref=rows_in.at[slot],
            send_sem=rows_ssem.at[index],
            recv_sem=rows_rsem.at[slot],
            device_id=(rows_target(index), col),
            device_id_type=MESH,
        )

    def rows_start(index):
        @pl.when(rows_target(index) != row)
        def _():
            rows_copy(index).start()

        @pl.when(rows_target(index) == row)
        def _():
            rows_in[slot] = z_in[index]

    loop(0, DEPTH, rows_start)

    loop(1, PLANE, lambda d: ag_copy(d).wait_recv())
    own_half = image.at[pl.ds(core * PLANE, PLANE)]
    fwd_copy = pltpu.make_async_remote_copy(
        src_ref=own_half,
        dst_ref=own_half,
        send_sem=fwd_send,
        recv_sem=fwd_recv,
        device_id=(other, col),
        device_id_type=MESH,
    )
    fwd_copy.start()
    reduce_middle(0)
    fwd_copy.wait_recv()

    columns = image.shape[0] * CHUNK

    def split_block(index):
        values = image[pl.ds(4 * index, 4)].reshape(4 * CHUNK, rank)
        high, low = split(values)
        window = pl.ds(pl.multiple_of(4 * CHUNK * index, 4 * CHUNK), 4 * CHUNK)
        right_out[window, 0:rank] = high
        right_out[window, rank : 2 * rank] = low
        right_out[window, 2 * rank : 3 * rank] = high

    loop(0, columns // (4 * CHUNK), split_block)

    def product_block(index):
        window = pl.ds(pl.multiple_of(256 * index, 256), 256)
        both = dot(a_high[window, :], right_out[:, 0 : 2 * rank])
        product[window, :] = (
            both[:, :rank] + both[:, rank:] + dot(a_low[window, :], right_out[:, 0:rank])
        )

    loop(0, product.shape[0] // 256, product_block)
    reduce_spread(0)

    def rows_wait(index):
        @pl.when(rows_source(index) != row)
        def _():
            pltpu.make_async_remote_copy(
                src_ref=z_in.at[index],
                dst_ref=rows_in.at[index],
                send_sem=rows_ssem.at[index],
                recv_sem=rows_rsem.at[index],
                device_id=(rows_source(index), col),
                device_id_type=MESH,
            ).wait_recv()

    loop(0, 8, rows_wait)
    row_image = rows_in[...].reshape(8 * CHUNK, rank)
    reduce_start(1, dot_split(row_image, product[...], TN))

    row_ids = lax.broadcasted_iota(jnp.int32, (rank, rank), 0)
    col_ids = lax.broadcasted_iota(jnp.int32, (rank, rank), 1)
    identity = jnp.where(row_ids == col_ids, 1.0, 0.0).astype(F32)
    gram = reduce_end(0)
    table[:, :rank] = gram
    table[:, rank:] = identity

    def eliminate(step):
        pivot_row = table[pl.ds(step, 1), :]
        left_part = table[:, :rank]
        column = jnp.sum(jnp.where(col_ids == step, left_part, 0.0), axis=1, keepdims=True)
        pivot = jnp.sum(
            jnp.where(col_ids[:1] == step, pivot_row[:, :rank], 0.0), axis=1, keepdims=True
        )
        factor = jnp.where(row_ids[:, :1] > step, column / pivot, 0.0)
        table[...] = table[...] - factor * pivot_row

    loop(0, 44, eliminate)
    reduce_middle(1)
    loop(44, 86, eliminate)
    reduce_spread(1)
    loop(86, rank, eliminate)
    pivots = jnp.sum(table[:, :rank] * identity, axis=1, keepdims=True)
    inverse = table[:, rank:] / jnp.sqrt(pivots)

    inner = reduce_end(1)
    raw_ritz = dot_full(dot_full(inverse, inner), inverse, NT)
    ritz = 0.5 * (raw_ritz + raw_ritz.T)
    square = dot_full(ritz, ritz) + 4.0 * penalty * identity
    frobenius = jnp.sqrt(jnp.sum(square * square, keepdims=True))

    pair[0:rank] = square / frobenius
    pair[rank:] = identity

    def newton(step):
        factor = 0.5 * (3.0 * identity - dot_split(pair[rank:], pair[0:rank]))
        pair[...] = dot_split(pair[...], factor)

    loop(0, NS_ITERS, newton)
    iterate = pair[0:rank]
    response = (ritz + jnp.sqrt(frobenius) * iterate) / (2.0 * penalty) - base_level * identity
    core_matrix = dot_full(dot_full(inverse, response, TN), inverse)
    weighted_high, weighted_low = split(dot_split(row_image, core_matrix))
    left_out[:, 0:rank] = weighted_high
    left_out[:, rank : 2 * rank] = weighted_high
    left_out[:, 2 * rank : 3 * rank] = weighted_low

    half_copy.wait_send()
    fwd_copy.wait_send()
    loop(1, PLANE, lambda d: rs_copy(d).wait_send())
    loop(1, PLANE, lambda d: ag_copy(d).wait_send())
    loop(1, DEPTH, lambda d: z_copy(d).wait_send())

    def rows_wait_send(index):
        @pl.when(rows_target(index) != row)
        def _():
            rows_copy(index).wait_send()

    loop(0, DEPTH, rows_wait_send)
    for which in range(2):
        loop(1, PLANE, lambda d: a_copy(which, d).wait_send())
        loop(1, 2 * DEPTH, lambda d: b_copy(which, d).wait_send())
        loop(1, PLANE, lambda d: c_copy(which, d).wait_send())


def solve(covariance, estimate, dual_var, start_basis):
    rows, cols = covariance.shape
    rank = start_basis.shape[1]
    vmem = pl.BlockSpec(memory_space=pltpu.VMEM)
    hbm = pl.BlockSpec(memory_space=pl.ANY)
    dma = pltpu.SemaphoreType.DMA
    chunk = (CHUNK, rank)
    return pl.pallas_call(
        solve_kernel,
        out_shape=(
            jax.ShapeDtypeStruct((rows, 3 * rank), BF16),
            jax.ShapeDtypeStruct((cols, 3 * rank), BF16),
        ),
        in_specs=[hbm, hbm, hbm, vmem],
        out_specs=(vmem, vmem),
        scratch_shapes=[
            pltpu.VMEM((rows, cols), BF16),
            pltpu.VMEM((rows, cols), BF16),
            pltpu.VMEM((rows, cols), BF16),
            pltpu.VMEM((rows, cols), BF16),
            pltpu.VMEM((rows, cols), BF16),
            pltpu.VMEM((PLANE, *chunk), F32),
            pltpu.VMEM((PLANE, *chunk), F32),
            pltpu.VMEM((PLANE, *chunk), F32),
            pltpu.VMEM((PLANE, *chunk), F32),
            pltpu.VMEM((PLANE, *chunk), F32),
            pltpu.VMEM((2 * PLANE, *chunk), F32),
            pltpu.VMEM((DEPTH, *chunk), F32),
            pltpu.VMEM((8, *chunk), F32),
            pltpu.VMEM((rows, rank), F32),
            pltpu.VMEM((2, PLANE, 8, rank), F32),
            pltpu.VMEM((2, PLANE, 8, rank), F32),
            pltpu.VMEM((2, 8, rank), F32),
            pltpu.VMEM((2, 2 * DEPTH, 8, rank), F32),
            pltpu.VMEM((2, PLANE, 8, rank), F32),
            pltpu.VMEM((rank, 2 * rank), F32),
            pltpu.VMEM((2 * rank, rank), F32),
            dma((3, 2)),
            dma,
            dma,
            dma((PLANE,)),
            dma((PLANE,)),
            dma((PLANE,)),
            dma((PLANE,)),
            dma,
            dma,
            dma((DEPTH,)),
            dma((DEPTH,)),
            dma((8,)),
            dma((8,)),
            dma((2, PLANE)),
            dma((2, PLANE)),
            dma((2, 2 * DEPTH)),
            dma((2, 2 * DEPTH)),
            dma((2, PLANE)),
            dma((2, PLANE)),
        ],
        compiler_params=pltpu.CompilerParams(
            collective_id=0, has_side_effects=True, vmem_limit_bytes=48 * 1024 * 1024
        ),
        name="solve",
    )(covariance, estimate, dual_var, start_basis)


def finish_kernel(left, right, dual, estimate_out, dual_out):
    width = dual.shape[1]
    theta = dot(left[...], right[...], NT)
    row_start = lax.axis_index("row") * theta.shape[0]
    col_start = lax.axis_index("col") * (width * pl.num_programs(0)) + pl.program_id(0) * width
    row_ids = lax.broadcasted_iota(jnp.int32, theta.shape, 0)
    col_ids = lax.broadcasted_iota(jnp.int32, theta.shape, 1)
    theta = theta + jnp.where(row_ids + (row_start - col_start) == col_ids, base_level, 0.0)
    mixture = theta + dual[...].astype(F32)
    clipped = jnp.clip(mixture, -threshold, threshold)
    estimate_out[...] = mixture - clipped
    dual_out[...] = clipped.astype(BF16)


def finish(left, right, dual_var):
    rows, cols = dual_var.shape
    width = 256
    depth = left.shape[1]
    tile = pl.BlockSpec((rows, width), lambda n: (0, n))
    return pl.pallas_call(
        finish_kernel,
        grid=(cols // width,),
        out_shape=(
            jax.ShapeDtypeStruct((rows, cols), F32),
            jax.ShapeDtypeStruct((rows, cols), BF16),
        ),
        in_specs=[
            pl.BlockSpec((rows, depth), lambda n: (0, 0)),
            pl.BlockSpec((width, depth), lambda n: (n, 0)),
            tile,
        ],
        out_specs=(tile, tile),
        name="finish",
    )(left, right, dual_var)


def body(covariance, estimate, dual_var, start_basis):
    left, right = solve(covariance, estimate, dual_var, start_basis)
    return finish(left, right, dual_var)


def solution(mesh):
    return jax.shard_map(
        body,
        mesh=mesh,
        in_specs=(P("row", "col"), P("row", "col"), P("row", "col"), P("row", None)),
        out_specs=(P("row", "col"), P("row", "col")),
        check_vma=False,
    )
```

time: 347 us -> 81.6 us (0.24)
  waiting for transfers between devices: 232 us -> 0 us
  Pallas kernels: 0 us -> 76.1 us
  matrix products: 42.2 us -> 0 us
  other arithmetic: 30 us -> 0 us
  starting transfers between devices: 18.1 us -> 0 us
  between operations: 14.9 us -> 0.66 us
    psum x1 -> x0, waiting for transfers between devices: 119 us -> none  [column_basis(): mapped = lax.psum(partial_terms, 'row')]
    all_to_all x3 -> x0, waiting for transfers between devices: 111 us -> none  [sent_to_all(): return lax.all_to_all(copies, axis, split_axis=0, concat_axis=0, tiled=True)]
    pallas_call x0 -> x2, Pallas kernels: none -> 76.1 us  [the longest x1 67.8 us: solve(): pl.pallas_call(solve_kernel, out_shape=(jax.ShapeDtypeStruct((rows, 3 * r...]
    dot_general x44 -> x0, matrix products: 41.9 us -> none  [the longest x1 9.96 us: column_basis(): lax.dot_general(shifted, row_basis, (((0,), (0,)), ((), ())), precision=h...]
    another operation x5 -> x0, other arithmetic: 22.9 us -> none  [the longest x3 12.4 us: normalize(): lower_factor = jnp.linalg.cholesky(gram_matrix)]
    all_to_all x3 -> x0, starting transfers between devices: 17.8 us -> none  [sent_to_all(): return lax.all_to_all(copies, axis, split_axis=0, concat_axis=0, tiled=True)]
    reduce_sum x3 -> x0, other arithmetic: 4.17 us -> none  [taken_together(): return jnp.sum(everything, axis=0)]
    broadcast_in_dim x3 -> x0, local copies, waits for them, and re-layouts: 3.84 us -> none  [sent_to_all(): copies = jnp.broadcast_to(array, (lax.axis_size(axis), *array.shape))]
  transfers between devices with their start and end apart: 5 -> 0, of which waited for: 5 -> 0; matrix products, arithmetic and copies ran while one was open for 1% -> 0% of each run, Pallas kernels for 0% -> 0%
where the time goes in v1:
time: 81.6 us; the launch traced here: 81.2 us
  Pallas kernels  76.1 us (93%)
  local copies, waits for them, and re-layouts  4.44 us (5%)
    pallas_call x1, Pallas kernels, solve(): pl.pallas_call(solve_kernel, out_shape=(jax.ShapeDtypeStruct((rows, 3 * r...  67.8 us
    pallas_call x1, Pallas kernels, finish(): pl.pallas_call(finish_kernel, grid=(cols // width,), out_shape=(jax.Shape...  8.37 us
    unnamed x8, local copies, waits for them, and re-layouts  4.44 us

profile of v1, /device:TPU:1, one launch (start us, length us, event | category | flops | bytes accessed | tf_op | source)
XLA Modules:
  0.0 81.2 jit_solution(9090829924285242564)
XLA Ops:
  0.6 0.0 copy-start
  0.6 1.6 %copy-done = bf16[512,2048]{1,0:T(8,128)(2,1)S(1)} copy-done((bf16[512,2048]{1,0:T(8,128)(2,1)S(1)}, bf16[512,2048]{1,0:T(8,128)(2,1)}, u32[]{:S(2)}) %copy-start) | copy-done | bytes 2097176
  2.2 0.0 copy-start.3
  2.2 0.9 %copy-done.3 = f32[512,128]{1,0:T(8,128)S(1)} copy-done((f32[512,128]{1,0:T(8,128)S(1)}, f32[512,128]{1,0:T(8,128)}, u32[]{:S(2)}) %copy-start.3) | copy-done | bytes 262168
  3.2 67.8 %solve.1 = (bf16[512,384]{1,0:T(8,128)(2,1)S(1)}, bf16[2048,384]{1,0:T(8,128)(2,1)S(1)}) custom-call(bf16[512,2048]{1,0:T(8,128)(2,1)S(1)} %copy-done, bf16[512,2048]{1,0:T(8,128)(2,1)} %est_hbm.1, bf16[512,2048]{1,0:T(8,128)(2,1)} %dual.1, f32[512,128]{1,0:T(8,128)S(1)} %copy-done.3), custom_call_target="tpu_custom_call" | custom-call | tf_op jit(solution)/shard_map/solve/pallas_call | solution.py:451
  71.0 0.0 copy-start.1
  71.0 1.2 %copy-done.1 = bf16[2048,384]{1,0:T(8,128)(2,1)} copy-done((bf16[2048,384]{1,0:T(8,128)(2,1)}, bf16[2048,384]{1,0:T(8,128)(2,1)S(1)}, u32[]{:S(2)}) %copy-start.1) | copy-done | bytes 1572888
  72.1 0.0 copy-start.2
  72.1 0.7 copy-done.2
  72.9 8.4 %finish.1 = (f32[512,2048]{1,0:T(8,128)}, bf16[512,2048]{1,0:T(8,128)(2,1)}) custom-call(bf16[512,384]{1,0:T(8,128)(2,1)} %copy-done.2, bf16[2048,384]{1,0:T(8,128)(2,1)} %copy-done.1, bf16[512,2048]{1,0:T(8,128)(2,1)} %dual.1), custom_call_target="tpu_custom_call" | custom-call | tf_op jit(solution)/shard_map/finish/pallas_call | solution.py:527
Async XLA Ops:
  0.6 1.6 %copy-start = (bf16[512,2048]{1,0:T(8,128)(2,1)S(1)}, bf16[512,2048]{1,0:T(8,128)(2,1)}, u32[]{:S(2)}) copy-start(bf16[512,2048]{1,0:T(8,128)(2,1)} %cov_hbm.1) | copy-start | bytes 6291460
  2.2 0.9 %copy-start.3 = (f32[512,128]{1,0:T(8,128)S(1)}, f32[512,128]{1,0:T(8,128)}, u32[]{:S(2)}) copy-start(f32[512,128]{1,0:T(8,128)} %basis.1) | copy-start | bytes 786436
  71.0 1.2 %copy-start.1 = (bf16[2048,384]{1,0:T(8,128)(2,1)}, bf16[2048,384]{1,0:T(8,128)(2,1)S(1)}, u32[]{:S(2)}) copy-start(bf16[2048,384]{1,0:T(8,128)(2,1)S(1)} %get-tuple-element.5.right) | copy-start | bytes 4718596
  72.1 0.7 copy-start.2

commit v2 on v1

v2 whole, which is shorter than its diff:
```python
import functools

import jax
import jax.numpy as jnp
from jax import lax
from jax.experimental import pallas as pl
from jax.experimental.pallas import tpu as pltpu
from jax.sharding import PartitionSpec as P

NS_ITERS = 12
MESH = pl.DeviceIdType.MESH
F32 = jnp.float32
BF16 = jnp.bfloat16

penalty = 0.01
threshold = 0.2
base_level = 10.0
highest = lax.Precision.HIGHEST

NN = (((1,), (0,)), ((), ()))
NT = (((1,), (1,)), ((), ()))
TN = (((0,), (0,)), ((), ()))

PLANE = 16
DEPTH = 8
CHUNK = 64
SOLVE_VMEM = 50500 * 1024
FINISH_VMEM = 32 * 1024 * 1024


def dot(left, right, dims=NN):
    return lax.dot_general(left, right, dims, preferred_element_type=F32)


def dot_full(left, right, dims=NN):
    return lax.dot_general(left, right, dims, precision=highest, preferred_element_type=F32)


def split(array):
    high = array.astype(BF16)
    return high, (array - high.astype(F32)).astype(BF16)


def dot_split(left, right, dims=NN):
    left_high, left_low = split(left)
    right_high, right_low = split(right)
    return dot(left_high, right_high, dims) + (
        dot(left_low, right_high, dims) + dot(left_high, right_low, dims)
    )


def loop(low, high, body):
    def step(index, carry):
        body(index)
        return carry

    lax.fori_loop(low, high, step, 0)


def arrived(ref, sem):
    pltpu.make_async_copy(ref, ref, sem).wait()


class Phase:
    def __init__(self):
        self.scope = None

    def __call__(self, name):
        if self.scope is not None:
            self.scope.__exit__(None, None, None)
        self.scope = None
        if name is not None:
            self.scope = jax.named_scope(name)
            self.scope.__enter__()


def solve_kernel(
    cov_hbm,
    est_hbm,
    dual_hbm,
    basis_hbm,
    left_out,
    right_out,
    dual,
    cov,
    est,
    basis,
    a_high,
    a_low,
    part_other,
    part_own,
    half_in,
    rs_send,
    rs_in,
    image,
    z_in,
    rows_in,
    product,
    red_part,
    red_in,
    red_mid,
    red_mid_in,
    red_out,
    table,
    load_sem,
    basis_sem,
    half_send,
    half_recv,
    rs_ssem,
    rs_rsem,
    ag_ssem,
    ag_rsem,
    fwd_send,
    fwd_recv,
    z_ssem,
    z_rsem,
    rows_ssem,
    rows_rsem,
    a_ssem,
    a_rsem,
    b_ssem,
    b_rsem,
    c_ssem,
    c_rsem,
):
    phase = Phase()
    phase("signal")
    row = lax.axis_index("row")
    col = lax.axis_index("col")
    core = lax.rem(row, 2)
    chip = lax.div(row, 2)
    other = row + 1 - 2 * core
    own_chunk = core * PLANE + chip
    own_line = lax.div(chip, 4)

    rank = basis.shape[1]
    width = 4 * CHUNK
    half = a_high.shape[1] // 2
    order = tuple(lax.rem(own_line + turn, 4) for turn in (2, 1, 3, 0))

    def window_of(side, block):
        offset = (1 - core if side == 0 else core) * half
        return pl.ds(pl.multiple_of(offset + block * width, width), width)

    def load(index, side, turn):
        source, target = ((cov_hbm, cov), (est_hbm, est), (dual_hbm, dual))[index]
        window = window_of(side, order[turn])
        return pltpu.make_async_copy(
            source.at[:, window], target.at[:, window], load_sem.at[index, side, turn]
        )

    basis_load = pltpu.make_async_copy(basis_hbm, basis, basis_sem)
    basis_load.start()
    for turn in range(4):
        for side in range(2):
            for index in range(3):
                load(index, side, turn).start()

    def plane_row(offset):
        return 2 * lax.rem(chip + offset, PLANE) + core

    def column_device(offset):
        target = lax.rem(2 * col + core + offset, 2 * DEPTH)
        return (2 * chip + lax.rem(target, 2), lax.div(target, 2))

    def rows_source(index):
        chunk = 8 * lax.rem(row, 4) + index
        return 2 * lax.rem(chunk, PLANE) + lax.div(chunk, PLANE)

    def rows_target(index):
        return 4 * index + lax.div(own_chunk, 8)

    barrier = pltpu.get_barrier_semaphore()

    def signal(device):
        pl.semaphore_signal(barrier, inc=1, device_id=device, device_id_type=MESH)

    loop(1, PLANE, lambda d: signal((plane_row(d), col)))
    loop(1, 2 * DEPTH, lambda d: signal(column_device(d)))

    def signal_source(index):
        source = rows_source(index)

        @pl.when(source != row)
        def _():
            signal((source, col))

    loop(0, 8, signal_source)

    has_own = lax.rem(row, 4) == lax.div(own_chunk, 8)
    peers = PLANE - 1 + 2 * DEPTH - 1 + 8 - jnp.where(has_own, 1, 0)

    phase("first")
    basis_load.wait()
    flipped = basis[...].T
    flip_high, flip_low = split(flipped)
    flip_both = jnp.concatenate([flip_high, flip_low], axis=0)

    def partial_terms(side, turn, target):
        for index in range(3):
            load(index, side, turn).wait()
        window = window_of(side, order[turn])
        shifted = penalty * (
            est[:, window].astype(F32) - dual[:, window].astype(F32)
        ) - cov[:, window].astype(F32)
        high, low = split(shifted)
        a_high[:, window] = high
        a_low[:, window] = low
        both = dot(flip_both, high)
        terms = both[:rank] + both[rank:] + dot(flip_high, low)
        target[pl.ds(4 * order[turn], 4)] = terms.T.reshape(4, CHUNK, rank)

    def half_copy(turn):
        block = pl.ds(4 * order[turn], 4)
        return pltpu.make_async_remote_copy(
            src_ref=part_other.at[block],
            dst_ref=half_in.at[block],
            send_sem=half_send.at[turn],
            recv_sem=half_recv.at[turn],
            device_id=(other, col),
            device_id_type=MESH,
        )

    def rs_copy(target):
        return pltpu.make_async_remote_copy(
            src_ref=rs_send.at[target],
            dst_ref=rs_in.at[chip],
            send_sem=rs_ssem,
            recv_sem=rs_rsem,
            device_id=(2 * target + core, col),
            device_id_type=MESH,
        )

    def combine(turn):
        half_copy(turn).wait_recv()
        block = pl.ds(4 * order[turn], 4)
        rs_send[block] = part_own[block] + half_in[block]

        def send(index):
            target = 4 * order[turn] + index

            @pl.when(target != chip)
            def _():
                rs_copy(target).start()

        loop(0, 4, send)

    for turn in range(4):
        partial_terms(0, turn, part_other)
        if turn == 0:
            phase("barrier")
            pl.semaphore_wait(barrier, peers)
            phase("second")
        half_copy(turn).start()
        partial_terms(1, turn, part_own)
        if turn > 0:
            combine(turn - 1)
    combine(3)
    rs_in[chip] = rs_send[chip]
    phase("rs_wait")
    arrived(rs_in.at[pl.ds(0, PLANE - 1)], rs_rsem)
    phase("spread")
    total = rs_in[0]
    for d in range(1, PLANE):
        total = total + rs_in[d]
    image[own_chunk] = total
    z_in[col] = total

    def z_copy(d):
        return pltpu.make_async_remote_copy(
            src_ref=image.at[own_chunk],
            dst_ref=z_in.at[col],
            send_sem=z_ssem,
            recv_sem=z_rsem,
            device_id=(row, lax.rem(col + d, DEPTH)),
            device_id_type=MESH,
        )

    def ag_copy(d):
        return pltpu.make_async_remote_copy(
            src_ref=image.at[own_chunk],
            dst_ref=image.at[own_chunk],
            send_sem=ag_ssem,
            recv_sem=ag_rsem,
            device_id=(plane_row(d), col),
            device_id_type=MESH,
        )

    def a_copy(which, d):
        return pltpu.make_async_remote_copy(
            src_ref=red_part.at[which, lax.rem(chip + d, PLANE)],
            dst_ref=red_in.at[which, chip],
            send_sem=a_ssem.at[which],
            recv_sem=a_rsem.at[which],
            device_id=(plane_row(d), col),
            device_id_type=MESH,
        )

    def b_copy(which, d):
        return pltpu.make_async_remote_copy(
            src_ref=red_mid.at[which],
            dst_ref=red_mid_in.at[which, 2 * col + core],
            send_sem=b_ssem.at[which],
            recv_sem=b_rsem.at[which],
            device_id=column_device(d),
            device_id_type=MESH,
        )

    def c_copy(which, d):
        return pltpu.make_async_remote_copy(
            src_ref=red_out.at[which, chip],
            dst_ref=red_out.at[which, chip],
            send_sem=c_ssem.at[which],
            recv_sem=c_rsem.at[which],
            device_id=(plane_row(d), col),
            device_id_type=MESH,
        )

    def reduce_start(which, value):
        red_part[which] = value.reshape(PLANE, 8, rank)
        loop(1, PLANE, lambda d: a_copy(which, d).start())
        red_in[which, chip] = red_part[which, chip]

    def reduce_middle(which):
        arrived(red_in.at[which, pl.ds(0, PLANE - 1)], a_rsem.at[which])
        piece = red_in[which, 0]
        for d in range(1, PLANE):
            piece = piece + red_in[which, d]
        red_mid[which] = piece
        red_mid_in[which, 2 * col + core] = piece
        loop(1, 2 * DEPTH, lambda d: b_copy(which, d).start())

    def reduce_spread(which):
        arrived(red_mid_in.at[which, pl.ds(0, 2 * DEPTH - 1)], b_rsem.at[which])
        piece = red_mid_in[which, 0]
        for d in range(1, 2 * DEPTH):
            piece = piece + red_mid_in[which, d]
        red_out[which, chip] = piece
        loop(1, PLANE, lambda d: c_copy(which, d).start())

    def reduce_end(which):
        arrived(red_out.at[which, pl.ds(0, PLANE - 1)], c_rsem.at[which])
        return red_out[which].reshape(rank, rank)

    loop(1, DEPTH, lambda d: z_copy(d).start())
    reduce_start(0, dot_full(total, total, TN))
    loop(1, PLANE, lambda d: ag_copy(d).start())
    phase("g_mid")
    reduce_middle(0)

    phase("z_wait")
    arrived(z_in.at[pl.ds(0, DEPTH - 1)], z_rsem)
    phase("rows_send")
    slot = lax.rem(own_chunk, 8)

    def rows_copy(index):
        return pltpu.make_async_remote_copy(
            src_ref=z_in.at[index],
            dst_ref=rows_in.at[slot],
            send_sem=rows_ssem.at[index],
            recv_sem=rows_rsem.at[slot],
            device_id=(rows_target(index), col),
            device_id_type=MESH,
        )

    def rows_start(index):
        @pl.when(rows_target(index) != row)
        def _():
            rows_copy(index).start()

        @pl.when(rows_target(index) == row)
        def _():
            rows_in[slot] = z_in[index]

    loop(0, DEPTH, rows_start)

    phase("ag_wait")
    arrived(image.at[pl.ds(0, PLANE - 1)], ag_rsem)
    phase("product1")
    own_half = image.at[pl.ds(core * PLANE, PLANE)]
    fwd_copy = pltpu.make_async_remote_copy(
        src_ref=own_half,
        dst_ref=own_half,
        send_sem=fwd_send,
        recv_sem=fwd_recv,
        device_id=(other, col),
        device_id_type=MESH,
    )
    fwd_copy.start()

    def product_terms(side):
        which = core if side == 0 else 1 - core

        def split_block(index):
            values = image[pl.ds(which * PLANE + 4 * index, 4)].reshape(width, rank)
            high, low = split(values)
            window = pl.ds(pl.multiple_of(which * half + width * index, width), width)
            right_out[window, 0:rank] = high
            right_out[window, rank : 2 * rank] = low
            right_out[window, 2 * rank : 3 * rank] = high

        loop(0, half // width, split_block)
        inner = pl.ds(pl.multiple_of(which * half, half), half)

        def product_block(index):
            window = pl.ds(pl.multiple_of(256 * index, 256), 256)
            both = dot(a_high[window, inner], right_out[inner, 0 : 2 * rank])
            terms = both[:, :rank] + (
                both[:, rank:] + dot(a_low[window, inner], right_out[inner, 0:rank])
            )
            product[window, :] = terms if side == 0 else product[window, :] + terms

        loop(0, product.shape[0] // 256, product_block)

    product_terms(0)
    phase("fwd_wait")
    fwd_copy.wait_recv()
    phase("product2")
    product_terms(1)
    phase("g_spread")
    reduce_spread(0)

    def rows_wait(index):
        @pl.when(rows_source(index) != row)
        def _():
            pltpu.make_async_remote_copy(
                src_ref=z_in.at[index],
                dst_ref=rows_in.at[index],
                send_sem=rows_ssem.at[index],
                recv_sem=rows_rsem.at[index],
                device_id=(rows_source(index), col),
                device_id_type=MESH,
            ).wait_recv()

    phase("rows_wait")
    loop(0, 8, rows_wait)
    phase("h_part")
    row_image = rows_in[...].reshape(8 * CHUNK, rank)
    reduce_start(1, dot_split(row_image, product[...], TN))

    phase("g_end")
    row_ids = lax.broadcasted_iota(jnp.int32, (rank, rank), 0)
    col_ids = lax.broadcasted_iota(jnp.int32, (rank, rank), 1)
    identity = jnp.where(row_ids == col_ids, 1.0, 0.0).astype(F32)
    gram = reduce_end(0)
    table[:, :rank] = gram
    table[:, rank:] = identity
    group = 4

    def lane_of(values, lane):
        return jnp.sum(
            jnp.where(col_ids[: values.shape[0]] == lane, values, 0.0), axis=1, keepdims=True
        )

    def eliminate(step):
        first = step * group
        pivot_rows = [table[pl.ds(first + p, 1), :] for p in range(group)]
        left_part = table[:, :rank]
        columns = [lane_of(left_part, first + p) for p in range(group)]
        entry = {
            (p, q): lane_of(pivot_rows[p][:, :rank], first + q)
            for p in range(group)
            for q in range(p, group)
        }
        change = None
        for p in range(group):
            scale = 1.0 / entry[p, p]
            factor = jnp.where(row_ids[:, :1] > first + p, columns[p] * scale, 0.0)
            for q in range(p + 1, group):
                columns[q] = columns[q] - factor * entry[p, q]
                weight = entry[p, q] * scale
                pivot_rows[q] = pivot_rows[q] - weight * pivot_rows[p]
                for t in range(q, group):
                    entry[q, t] = entry[q, t] - weight * entry[p, t]
            term = factor * pivot_rows[p]
            change = term if change is None else change + term
        table[...] = table[...] - change

    phase("elim1")
    loop(0, 6, eliminate)
    phase("h_mid")
    reduce_middle(1)
    phase("elim2")
    loop(6, 22, eliminate)
    phase("h_spread")
    reduce_spread(1)
    phase("elim3")
    loop(22, rank // group, eliminate)
    pivots = jnp.sum(table[:, :rank] * identity, axis=1, keepdims=True)
    inverse = table[:, rank:] / jnp.sqrt(pivots)
    row_basis = dot_split(row_image, inverse, NT)

    phase("drain")
    for turn in range(4):
        half_copy(turn).wait_send()
    fwd_copy.wait_send()
    arrived(rs_send.at[pl.ds(0, PLANE - 1)], rs_ssem)
    arrived(image.at[pl.ds(0, PLANE - 1)], ag_ssem)
    arrived(z_in.at[pl.ds(0, DEPTH - 1)], z_ssem)

    def rows_wait_send(index):
        @pl.when(rows_target(index) != row)
        def _():
            rows_copy(index).wait_send()

    loop(0, DEPTH, rows_wait_send)

    phase("h_end")
    inner = reduce_end(1)
    phase("ritz")
    raw_ritz = dot_split(dot_split(inverse, inner), inverse, NT)
    ritz = 0.5 * (raw_ritz + raw_ritz.T)
    square = dot_split(ritz, ritz) + 4.0 * penalty * identity
    frobenius = jnp.sqrt(jnp.sum(square * square, keepdims=True))

    phase("newton")
    iterate = square / frobenius
    both = iterate
    for _ in range(NS_ITERS):
        factor = 0.5 * (3.0 * identity - both)
        factor_high, factor_low = split(factor)
        factor_both = jnp.concatenate([factor_high, factor_low], axis=1)

        def scaled(left, factor_both=factor_both, factor_high=factor_high):
            high, low = split(left)
            terms = dot(high, factor_both)
            return terms[:, :rank] + (terms[:, rank:] + dot(low, factor_high))

        both = scaled(scaled(both))
        iterate = scaled(iterate)
    phase("tail")
    response = (ritz + jnp.sqrt(frobenius) * iterate) / (2.0 * penalty) - base_level * identity
    weighted_high, weighted_low = split(dot_split(row_basis, dot_split(response, inverse)))
    left_out[:, 0:rank] = weighted_high
    left_out[:, rank : 2 * rank] = weighted_high
    left_out[:, 2 * rank : 3 * rank] = weighted_low
    for which in range(2):
        arrived(red_in.at[which, pl.ds(0, PLANE - 1)], a_ssem.at[which])
        arrived(red_mid_in.at[which, pl.ds(0, 2 * DEPTH - 1)], b_ssem.at[which])
        arrived(red_out.at[which, pl.ds(0, PLANE - 1)], c_ssem.at[which])
    phase(None)


def solve(covariance, estimate, dual_var, start_basis):
    rows, cols = covariance.shape
    rank = start_basis.shape[1]
    vmem = pl.BlockSpec(memory_space=pltpu.VMEM)
    hbm = pl.BlockSpec(memory_space=pltpu.HBM)
    dma = pltpu.SemaphoreType.DMA
    matrix = pltpu.VMEM((rows, cols), BF16)
    chunk = (CHUNK, rank)
    chunks = pltpu.VMEM((PLANE, *chunk), F32)
    pieces = pltpu.VMEM((2, PLANE, 8, rank), F32)
    return pl.pallas_call(
        solve_kernel,
        out_shape=(
            jax.ShapeDtypeStruct((rows, 3 * rank), BF16),
            jax.ShapeDtypeStruct((cols, 3 * rank), BF16),
            jax.ShapeDtypeStruct((rows, cols), BF16),
        ),
        in_specs=[hbm, hbm, hbm, hbm],
        out_specs=(vmem, vmem, vmem),
        scratch_shapes=[
            matrix,
            matrix,
            pltpu.VMEM((rows, rank), F32),
            matrix,
            matrix,
            chunks,
            chunks,
            chunks,
            chunks,
            chunks,
            pltpu.VMEM((2 * PLANE, *chunk), F32),
            pltpu.VMEM((DEPTH, *chunk), F32),
            pltpu.VMEM((8, *chunk), F32),
            pltpu.VMEM((rows, rank), F32),
            pieces,
            pieces,
            pltpu.VMEM((2, 8, rank), F32),
            pieces,
            pieces,
            pltpu.VMEM((rank, 2 * rank), F32),
            dma((3, 2, 4)),
            dma,
            dma((4,)),
            dma((4,)),
            dma,
            dma,
            dma,
            dma,
            dma,
            dma,
            dma,
            dma,
            dma((8,)),
            dma((8,)),
            dma((2,)),
            dma((2,)),
            dma((2,)),
            dma((2,)),
            dma((2,)),
            dma((2,)),
        ],
        compiler_params=pltpu.CompilerParams(
            collective_id=0, has_side_effects=True, vmem_limit_bytes=SOLVE_VMEM
        ),
        name="solve",
    )(covariance, estimate, dual_var, start_basis)


def finish_kernel(left, right, dual, estimate_hbm, dual_hbm, estimate_out, dual_out, out_sem):
    rows, cols = dual.shape
    width = rows
    row = lax.axis_index("row")
    on_diagonal = lax.div(row, cols // rows) == lax.axis_index("col")
    row_ids = lax.broadcasted_iota(jnp.int32, (rows, width), 0)
    col_ids = lax.broadcasted_iota(jnp.int32, (rows, width), 1)

    def copies(block):
        window = pl.ds(pl.multiple_of(block * width, width), width)
        return (
            pltpu.make_async_copy(
                estimate_out.at[:, window], estimate_hbm.at[:, window], out_sem.at[0, block]
            ),
            pltpu.make_async_copy(
                dual_out.at[:, window], dual_hbm.at[:, window], out_sem.at[1, block]
            ),
        )

    def tile(block):
        window = pl.ds(pl.multiple_of(block * width, width), width)
        theta = dot(left[...], right[pl.ds(pl.multiple_of(block * width, width), width), :], NT)
        level = jnp.where(
            on_diagonal & (block == lax.rem(row, cols // rows)), base_level, 0.0
        ).astype(F32)
        theta = theta + jnp.where(row_ids == col_ids, level, 0.0)
        mixture = theta + dual[:, window].astype(F32)
        clipped = jnp.clip(mixture, -threshold, threshold)
        estimate_out[:, window] = mixture - clipped
        dual_out[:, window] = clipped.astype(BF16)
        for copy in copies(block):
            copy.start()

    loop(0, cols // width, tile)
    for block in range(cols // width):
        for copy in copies(block):
            copy.wait()


def finish(left, right, dual_var):
    rows, cols = dual_var.shape
    vmem = pl.BlockSpec(memory_space=pltpu.VMEM)
    hbm = pl.BlockSpec(memory_space=pltpu.HBM)
    return pl.pallas_call(
        finish_kernel,
        out_shape=(
            jax.ShapeDtypeStruct((rows, cols), F32),
            jax.ShapeDtypeStruct((rows, cols), BF16),
        ),
        in_specs=[vmem, vmem, vmem],
        out_specs=(hbm, hbm),
        scratch_shapes=[
            pltpu.VMEM((rows, cols), F32),
            pltpu.VMEM((rows, cols), BF16),
            pltpu.SemaphoreType.DMA((2, cols // rows)),
        ],
        compiler_params=pltpu.CompilerParams(vmem_limit_bytes=FINISH_VMEM),
        name="finish",
    )(left, right, dual_var)


def body(covariance, estimate, dual_var, start_basis):
    left, right, dual_kept = solve(covariance, estimate, dual_var, start_basis)
    return finish(left, right, dual_kept)


def solution(mesh):
    return jax.shard_map(
        body,
        mesh=mesh,
        in_specs=(P("row", "col"), P("row", "col"), P("row", "col"), P("row", None)),
        out_specs=(P("row", "col"), P("row", "col")),
        check_vma=False,
    )
```

time: 81.6 us -> 61.7 us (0.76)
  Pallas kernels: 76.1 us -> 60 us
  local copies, waits for them, and re-layouts: 4.44 us -> 0.94 us
    pallas_call x1, Pallas kernels: 67.8 us -> 56.6 us  [solve(): pl.pallas_call(solve_kernel, out_shape=(jax.ShapeDtypeStruct((rows, 3 * r...]
    pallas_call x1, Pallas kernels: 8.37 us -> 3.36 us  [finish(): pl.pallas_call(finish_kernel, out_shape=(jax.ShapeDtypeStruct((rows, cols...]
    unnamed x8 -> x2, local copies, waits for them, and re-layouts: 4.44 us -> 0.94 us
where the time goes in v2:
time: 61.7 us; the launch traced here: 61.6 us
  Pallas kernels  60 us (97%)
  local copies, waits for them, and re-layouts  0.94 us (2%)
  between operations  0.65 us (1%)
    pallas_call x1, Pallas kernels, solve(): pl.pallas_call(solve_kernel, out_shape=(jax.ShapeDtypeStruct((rows, 3 * r...  56.6 us
    pallas_call x1, Pallas kernels, finish(): pl.pallas_call(finish_kernel, out_shape=(jax.ShapeDtypeStruct((rows, cols...  3.36 us

profile of v2, /device:TPU:1, one launch (start us, length us, event | category | flops | bytes accessed | tf_op | source)
XLA Modules:
  0.0 61.6 jit_solution(4448912183618940621)
XLA Ops:
  0.6 0.0 copy-start
  0.6 0.9 %copy-done = f32[512,128]{1,0:T(8,128)S(1)} copy-done((f32[512,128]{1,0:T(8,128)S(1)}, f32[512,128]{1,0:T(8,128)}, u32[]{:S(2)}) %copy-start) | copy-done | bytes 262168
  1.6 56.6 %solve.1 = (bf16[512,384]{1,0:T(8,128)(2,1)S(1)}, bf16[2048,384]{1,0:T(8,128)(2,1)S(1)}, bf16[512,2048]{1,0:T(8,128)(2,1)S(1)}) custom-call(bf16[512,2048]{1,0:T(8,128)(2,1)} %cov_hbm.1, bf16[512,2048]{1,0:T(8,128)(2,1)} %est_hbm.1, bf16[512,2048]{1,0:T(8,128)(2,1)} %dual_hbm.1, f32[512,128]{1,0:T(8,128)S(1)} %copy-done), custom_call_target="tpu_custom_call" | custom-call | tf_op jit(solution)/shard_map/solve/pallas_call | solution.py:554
  58.2 3.4 %finish.1 = (f32[512,2048]{1,0:T(8,128)}, bf16[512,2048]{1,0:T(8,128)(2,1)}) custom-call(bf16[512,384]{1,0:T(8,128)(2,1)S(1)} %get-tuple-element.5.left, bf16[2048,384]{1,0:T(8,128)(2,1)S(1)} %get-tuple-element.6.right, bf16[512,2048]{1,0:T(8,128)(2,1)S(1)} %get-tuple-element.7.dual), custom_call_target="tpu_custom_call" | custom-call | tf_op jit(solution)/shard_map/finish/pallas_call | solution.py:655
Async XLA Ops:
  0.6 1.0 %copy-start = (f32[512,128]{1,0:T(8,128)S(1)}, f32[512,128]{1,0:T(8,128)}, u32[]{:S(2)}) copy-start(f32[512,128]{1,0:T(8,128)} %basis_hbm.1) | copy-start | bytes 786436

commit v3 on v2

--- a/solution.py
+++ b/solution.py
@@ -24,6 +24,24 @@
 PLANE = 16
 DEPTH = 8
 CHUNK = 64
+PARTS = 2
+PART = CHUNK // PARTS
+
+
+def ring(offset, size):
+    return min(offset, size - offset)
+
+
+PLANE_OFFSETS = sorted(
+    ((dy, dx) for dy in range(4) for dx in range(4) if dy or dx),
+    key=lambda o: -(ring(o[0], 4) + ring(o[1], 4)),
+)
+SHIFTS = (2, 1, 3, 0)
+DEPTH_OFFSETS = sorted(range(1, DEPTH), key=lambda d: -ring(d, DEPTH))
+COLUMN_OFFSETS = sorted(
+    ((dz, dc) for dz in range(DEPTH) for dc in range(2) if dz or dc),
+    key=lambda o: -(ring(o[0], DEPTH) + 0.5 * o[1]),
+)
 SOLVE_VMEM = 50500 * 1024
 FINISH_VMEM = 32 * 1024 * 1024
 
@@ -135,33 +153,34 @@
 
     rank = basis.shape[1]
     width = 4 * CHUNK
-    half = a_high.shape[1] // 2
-    order = tuple(lax.rem(own_line + turn, 4) for turn in (2, 1, 3, 0))
-
-    def window_of(side, block):
-        offset = (1 - core if side == 0 else core) * half
-        return pl.ds(pl.multiple_of(offset + block * width, width), width)
-
-    def load(index, side, turn):
+    half = 4 * width
+
+    def load(index, side, shift):
         source, target = ((cov_hbm, cov), (est_hbm, est), (dual_hbm, dual))[index]
-        window = window_of(side, order[turn])
+        offset = (1 - core if side == 0 else core) * half + lax.rem(own_line + shift, 4) * width
+        window = pl.ds(pl.multiple_of(offset, width), width)
         return pltpu.make_async_copy(
-            source.at[:, window], target.at[:, window], load_sem.at[index, side, turn]
+            source.at[:, window], target.at[4 * side + shift], load_sem.at[index, side, shift]
         )
 
     basis_load = pltpu.make_async_copy(basis_hbm, basis, basis_sem)
     basis_load.start()
-    for turn in range(4):
+    for shift in SHIFTS:
         for side in range(2):
             for index in range(3):
-                load(index, side, turn).start()
-
-    def plane_row(offset):
-        return 2 * lax.rem(chip + offset, PLANE) + core
+                load(index, side, shift).start()
+
+    def plane_chip(offset):
+        dy, dx = offset
+        return 4 * lax.rem(own_line + dy, 4) + lax.rem(lax.rem(chip, 4) + dx, 4)
+
+    plane_chips = [plane_chip(offset) for offset in PLANE_OFFSETS]
 
     def column_device(offset):
-        target = lax.rem(2 * col + core + offset, 2 * DEPTH)
-        return (2 * chip + lax.rem(target, 2), lax.div(target, 2))
+        dz, dc = offset
+        return (2 * chip + lax.rem(core + dc, 2), lax.rem(col + dz, DEPTH))
+
+    column_devices = [column_device(offset) for offset in COLUMN_OFFSETS]
 
     def rows_source(index):
         chunk = 8 * lax.rem(row, 4) + index
@@ -175,8 +194,10 @@
     def signal(device):
         pl.semaphore_signal(barrier, inc=1, device_id=device, device_id_type=MESH)
 
-    loop(1, PLANE, lambda d: signal((plane_row(d), col)))
-    loop(1, 2 * DEPTH, lambda d: signal(column_device(d)))
+    for target in plane_chips:
+        signal((2 * target + core, col))
+    for device in column_devices:
+        signal(device)
 
     def signal_source(index):
         source = rows_source(index)
@@ -196,129 +217,132 @@
     flip_high, flip_low = split(flipped)
     flip_both = jnp.concatenate([flip_high, flip_low], axis=0)
 
-    def partial_terms(side, turn, target):
-        for index in range(3):
-            load(index, side, turn).wait()
-        window = window_of(side, order[turn])
-        shifted = penalty * (
-            est[:, window].astype(F32) - dual[:, window].astype(F32)
-        ) - cov[:, window].astype(F32)
-        high, low = split(shifted)
-        a_high[:, window] = high
-        a_low[:, window] = low
-        both = dot(flip_both, high)
-        terms = both[:rank] + both[rank:] + dot(flip_high, low)
-        target[pl.ds(4 * order[turn], 4)] = terms.T.reshape(4, CHUNK, rank)
-
-    def half_copy(turn):
-        block = pl.ds(4 * order[turn], 4)
+    def load_wait(shift):
+        for side in range(2):
+            for index in range(3):
+                load(index, side, shift).wait()
+
+    def partial_terms(shift):
+        for side, target in ((0, part_other), (1, part_own)):
+            slot = 4 * side + shift
+            shifted = penalty * (est[slot].astype(F32) - dual[slot].astype(F32)) - cov[slot].astype(F32)
+            high, low = split(shifted)
+            a_high[slot] = high
+            a_low[slot] = low
+            both = dot(flip_both, high)
+            terms = both[:rank] + (both[rank:] + dot(flip_high, low))
+            target[4 * shift : 4 * shift + 4] = terms.T.reshape(4, CHUNK, rank)
+
+    part_rows = [pl.ds(PART * part, PART) for part in range(PARTS)]
+
+    def half_copy(shift):
+        block = pl.ds(4 * shift, 4)
         return pltpu.make_async_remote_copy(
             src_ref=part_other.at[block],
             dst_ref=half_in.at[block],
-            send_sem=half_send.at[turn],
-            recv_sem=half_recv.at[turn],
+            send_sem=half_send.at[shift],
+            recv_sem=half_recv.at[shift],
             device_id=(other, col),
             device_id_type=MESH,
         )
 
-    def rs_copy(target):
-        return pltpu.make_async_remote_copy(
-            src_ref=rs_send.at[target],
-            dst_ref=rs_in.at[chip],
+    def rs_copy(part, place, target):
+        return pltpu.make_async_remote_copy(
+            src_ref=rs_send.at[place, part_rows[part]],
+            dst_ref=rs_in.at[part, chip],
             send_sem=rs_ssem,
-            recv_sem=rs_rsem,
+            recv_sem=rs_rsem.at[part],
             device_id=(2 * target + core, col),
             device_id_type=MESH,
         )
 
-    def combine(turn):
-        half_copy(turn).wait_recv()
-        block = pl.ds(4 * order[turn], 4)
+    def send_terms(part, shift):
+        for turn in (2, 1, 3, 0):
+            if shift or turn:
+                place = 4 * shift + lax.rem(lax.rem(chip, 4) + turn, 4)
+                target = 4 * lax.rem(own_line + shift, 4) + lax.rem(lax.rem(chip, 4) + turn, 4)
+                rs_copy(part, place, target).start()
+
+    def combine(shift):
+        half_copy(shift).wait_recv()
+        block = slice(4 * shift, 4 * shift + 4)
         rs_send[block] = part_own[block] + half_in[block]
-
-        def send(index):
-            target = 4 * order[turn] + index
-
-            @pl.when(target != chip)
-            def _():
-                rs_copy(target).start()
-
-        loop(0, 4, send)
-
-    for turn in range(4):
-        partial_terms(0, turn, part_other)
-        if turn == 0:
-            phase("barrier")
-            pl.semaphore_wait(barrier, peers)
-            phase("second")
-        half_copy(turn).start()
-        partial_terms(1, turn, part_own)
-        if turn > 0:
-            combine(turn - 1)
-    combine(3)
-    rs_in[chip] = rs_send[chip]
-    phase("rs_wait")
-    arrived(rs_in.at[pl.ds(0, PLANE - 1)], rs_rsem)
-    phase("spread")
-    total = rs_in[0]
-    for d in range(1, PLANE):
-        total = total + rs_in[d]
-    image[own_chunk] = total
-    z_in[col] = total
-
-    def z_copy(d):
-        return pltpu.make_async_remote_copy(
-            src_ref=image.at[own_chunk],
-            dst_ref=z_in.at[col],
+        send_terms(0, shift)
+
+    load_wait(SHIFTS[0])
+    partial_terms(SHIFTS[0])
+    phase("barrier")
+    pl.semaphore_wait(barrier, peers)
+    phase("second")
+    half_copy(SHIFTS[0]).start()
+    for shift in SHIFTS[1:]:
+        load_wait(shift)
+    for turn in range(1, 4):
+        partial_terms(SHIFTS[turn])
+        half_copy(SHIFTS[turn]).start()
+        if turn > 1:
+            combine(SHIFTS[turn - 2])
+    phase("last")
+    combine(SHIFTS[2])
+    combine(SHIFTS[3])
+    for part in range(1, PARTS):
+        for shift in SHIFTS:
+            send_terms(part, shift)
+    own_place = lax.rem(chip, 4)
+    def z_copy(part, d):
+        return pltpu.make_async_remote_copy(
+            src_ref=image.at[own_chunk, part_rows[part]],
+            dst_ref=z_in.at[col, part_rows[part]],
             send_sem=z_ssem,
-            recv_sem=z_rsem,
+            recv_sem=z_rsem.at[part, d],
             device_id=(row, lax.rem(col + d, DEPTH)),
             device_id_type=MESH,
         )
 
-    def ag_copy(d):
-        return pltpu.make_async_remote_copy(
-            src_ref=image.at[own_chunk],
-            dst_ref=image.at[own_chunk],
+    def ag_copy(part, target, lines):
+        return pltpu.make_async_remote_copy(
+            src_ref=image.at[own_chunk, part_rows[part]],
+            dst_ref=image.at[own_chunk, part_rows[part]],
             send_sem=ag_ssem,
-            recv_sem=ag_rsem,
-            device_id=(plane_row(d), col),
-            device_id_type=MESH,
-        )
-
-    def a_copy(which, d):
-        return pltpu.make_async_remote_copy(
-            src_ref=red_part.at[which, lax.rem(chip + d, PLANE)],
+            recv_sem=ag_rsem.at[lines],
+            device_id=(2 * target + core, col),
+            device_id_type=MESH,
+        )
+
+    def a_copy(which, target):
+        return pltpu.make_async_remote_copy(
+            src_ref=red_part.at[which, target],
             dst_ref=red_in.at[which, chip],
             send_sem=a_ssem.at[which],
             recv_sem=a_rsem.at[which],
-            device_id=(plane_row(d), col),
-            device_id_type=MESH,
-        )
-
-    def b_copy(which, d):
+            device_id=(2 * target + core, col),
+            device_id_type=MESH,
+        )
+
+    def b_copy(which, device):
         return pltpu.make_async_remote_copy(
             src_ref=red_mid.at[which],
             dst_ref=red_mid_in.at[which, 2 * col + core],
             send_sem=b_ssem.at[which],
             recv_sem=b_rsem.at[which],
-            device_id=column_device(d),
-            device_id_type=MESH,
-        )
-
-    def c_copy(which, d):
+            device_id=device,
+            device_id_type=MESH,
+        )
+
+    def c_copy(which, target):
         return pltpu.make_async_remote_copy(
             src_ref=red_out.at[which, chip],
             dst_ref=red_out.at[which, chip],
             send_sem=c_ssem.at[which],
             recv_sem=c_rsem.at[which],
-            device_id=(plane_row(d), col),
+            device_id=(2 * target + core, col),
             device_id_type=MESH,
         )
 
     def reduce_start(which, value):
         red_part[which] = value.reshape(PLANE, 8, rank)
-        loop(1, PLANE, lambda d: a_copy(which, d).start())
+        for target in plane_chips:
+            a_copy(which, target).start()
         red_in[which, chip] = red_part[which, chip]
 
     def reduce_middle(which):
@@ -328,7 +352,8 @@
             piece = piece + red_in[which, d]
         red_mid[which] = piece
         red_mid_in[which, 2 * col + core] = piece
-        loop(1, 2 * DEPTH, lambda d: b_copy(which, d).start())
+        for device in column_devices:
+            b_copy(which, device).start()
 
     def reduce_spread(which):
         arrived(red_mid_in.at[which, pl.ds(0, 2 * DEPTH - 1)], b_rsem.at[which])
@@ -336,101 +361,123 @@
         for d in range(1, 2 * DEPTH):
             piece = piece + red_mid_in[which, d]
         red_out[which, chip] = piece
-        loop(1, PLANE, lambda d: c_copy(which, d).start())
+        for target in plane_chips:
+            c_copy(which, target).start()
 
     def reduce_end(which):
         arrived(red_out.at[which, pl.ds(0, PLANE - 1)], c_rsem.at[which])
         return red_out[which].reshape(rank, rank)
 
-    loop(1, DEPTH, lambda d: z_copy(d).start())
-    reduce_start(0, dot_full(total, total, TN))
-    loop(1, PLANE, lambda d: ag_copy(d).start())
-    phase("g_mid")
-    reduce_middle(0)
-
-    phase("z_wait")
-    arrived(z_in.at[pl.ds(0, DEPTH - 1)], z_rsem)
-    phase("rows_send")
+    for part in range(PARTS):
+        phase(f"rs_wait{part}")
+        arrived(rs_in.at[part, pl.ds(0, PLANE - 1)], rs_rsem.at[part])
+        phase(f"spread{part}")
+        rs_in[part, chip] = rs_send[own_place, part_rows[part]]
+        terms = rs_in[part, 0]
+        for d in range(1, PLANE):
+            terms = terms + rs_in[part, d]
+        image[own_chunk, part_rows[part]] = terms
+        z_in[col, part_rows[part]] = terms
+        for d in DEPTH_OFFSETS:
+            z_copy(part, d).start()
+        if part == PARTS - 1:
+            total = image[own_chunk]
+            reduce_start(0, dot_full(total, total, TN))
+        for offset, target in zip(PLANE_OFFSETS, plane_chips, strict=True):
+            ag_copy(part, target, offset[0]).start()
+
     slot = lax.rem(own_chunk, 8)
 
-    def rows_copy(index):
-        return pltpu.make_async_remote_copy(
-            src_ref=z_in.at[index],
-            dst_ref=rows_in.at[slot],
-            send_sem=rows_ssem.at[index],
-            recv_sem=rows_rsem.at[slot],
+    def rows_copy(part, index):
+        return pltpu.make_async_remote_copy(
+            src_ref=z_in.at[index, part_rows[part]],
+            dst_ref=rows_in.at[slot, part_rows[part]],
+            send_sem=rows_ssem.at[part, index],
+            recv_sem=rows_rsem.at[part, slot],
             device_id=(rows_target(index), col),
             device_id_type=MESH,
         )
 
-    def rows_start(index):
+    def rows_start(part, index):
         @pl.when(rows_target(index) != row)
         def _():
-            rows_copy(index).start()
+            rows_copy(part, index).start()
 
         @pl.when(rows_target(index) == row)
         def _():
-            rows_in[slot] = z_in[index]
-
-    loop(0, DEPTH, rows_start)
-
-    phase("ag_wait")
-    arrived(image.at[pl.ds(0, PLANE - 1)], ag_rsem)
-    phase("product1")
-    own_half = image.at[pl.ds(core * PLANE, PLANE)]
-    fwd_copy = pltpu.make_async_remote_copy(
-        src_ref=own_half,
-        dst_ref=own_half,
-        send_sem=fwd_send,
-        recv_sem=fwd_recv,
-        device_id=(other, col),
-        device_id_type=MESH,
-    )
-    fwd_copy.start()
+            rows_in[slot, part_rows[part]] = z_in[index, part_rows[part]]
+
+    def forward(part, d):
+        arrived(z_in.at[0, part_rows[part]], z_rsem.at[part, d])
+        rows_start(part, lax.rem(col + DEPTH - d, DEPTH))
+
+    def fwd_copy(lines):
+        line = lax.rem(own_line + 4 - lines, 4)
+        chunks = image.at[pl.ds(core * PLANE + 4 * line, 4)]
+        return pltpu.make_async_remote_copy(
+            src_ref=chunks,
+            dst_ref=chunks,
+            send_sem=fwd_send.at[lines],
+            recv_sem=fwd_recv.at[lines],
+            device_id=(other, col),
+            device_id_type=MESH,
+        )
 
     def product_terms(side):
         which = core if side == 0 else 1 - core
-
-        def split_block(index):
-            values = image[pl.ds(which * PLANE + 4 * index, 4)].reshape(width, rank)
-            high, low = split(values)
-            window = pl.ds(pl.multiple_of(which * half + width * index, width), width)
+        highs, lows = [], []
+        for shift in range(4):
+            block = which * PLANE + 4 * lax.rem(own_line + shift, 4)
+            window = pl.ds(pl.multiple_of(block * CHUNK, width), width)
+            high, low = split(image[pl.ds(block, 4)].reshape(width, rank))
             right_out[window, 0:rank] = high
             right_out[window, rank : 2 * rank] = low
             right_out[window, 2 * rank : 3 * rank] = high
-
-        loop(0, half // width, split_block)
-        inner = pl.ds(pl.multiple_of(which * half, half), half)
-
-        def product_block(index):
-            window = pl.ds(pl.multiple_of(256 * index, 256), 256)
-            both = dot(a_high[window, inner], right_out[inner, 0 : 2 * rank])
+            highs.append(high)
+            lows.append(low)
+        right_high = jnp.concatenate(highs, axis=0)
+        right_both = jnp.concatenate([right_high, jnp.concatenate(lows, axis=0)], axis=1)
+        slots = range(4 * (1 - side), 4 * (1 - side) + 4)
+        for start in range(0, product.shape[0], 256):
+            rows = pl.ds(start, 256)
+            both = dot(jnp.concatenate([a_high[slot, rows] for slot in slots], axis=1), right_both)
             terms = both[:, :rank] + (
-                both[:, rank:] + dot(a_low[window, inner], right_out[inner, 0:rank])
+                both[:, rank:]
+                + dot(jnp.concatenate([a_low[slot, rows] for slot in slots], axis=1), right_high)
             )
-            product[window, :] = terms if side == 0 else product[window, :] + terms
-
-        loop(0, product.shape[0] // 256, product_block)
-
+            product[rows] = product[rows] + terms if side else terms
+
+    def line_in(lines):
+        count = 4 if lines else 3
+        arrived(image.at[pl.ds(0, count)], ag_rsem.at[lines])
+        fwd_copy(lines).start()
+
+    phase("z0")
+    for part in range(PARTS):
+        rows_start(part, col)
+    for d in DEPTH_OFFSETS:
+        forward(0, d)
+    phase("g_mid")
+    reduce_middle(0)
+    phase("z1")
+    for d in DEPTH_OFFSETS:
+        forward(1, d)
+    phase("lines")
+    for lines in (2, 1, 3, 0):
+        line_in(lines)
+    phase("product0")
     product_terms(0)
     phase("fwd_wait")
-    fwd_copy.wait_recv()
-    phase("product2")
+    for lines in range(4):
+        fwd_copy(lines).wait_recv()
+    phase("product1")
     product_terms(1)
-    phase("g_spread")
-    reduce_spread(0)
 
     def rows_wait(index):
         @pl.when(rows_source(index) != row)
         def _():
-            pltpu.make_async_remote_copy(
-                src_ref=z_in.at[index],
-                dst_ref=rows_in.at[index],
-                send_sem=rows_ssem.at[index],
-                recv_sem=rows_rsem.at[index],
-                device_id=(rows_source(index), col),
-                device_id_type=MESH,
-            ).wait_recv()
+            for part in range(PARTS):
+                arrived(rows_in.at[index, part_rows[part]], rows_rsem.at[part, index])
 
     phase("rows_wait")
     loop(0, 8, rows_wait)
@@ -438,13 +485,9 @@
     row_image = rows_in[...].reshape(8 * CHUNK, rank)
     reduce_start(1, dot_split(row_image, product[...], TN))
 
-    phase("g_end")
     row_ids = lax.broadcasted_iota(jnp.int32, (rank, rank), 0)
     col_ids = lax.broadcasted_iota(jnp.int32, (rank, rank), 1)
     identity = jnp.where(row_ids == col_ids, 1.0, 0.0).astype(F32)
-    gram = reduce_end(0)
-    table[:, :rank] = gram
-    table[:, rank:] = identity
     group = 4
 
     def lane_of(values, lane):
@@ -476,24 +519,28 @@
             change = term if change is None else change + term
         table[...] = table[...] - change
 
-    phase("elim1")
-    loop(0, 6, eliminate)
+    phase("g_spread")
+    reduce_spread(0)
     phase("h_mid")
     reduce_middle(1)
-    phase("elim2")
-    loop(6, 22, eliminate)
+    phase("g_end")
+    table[:, :rank] = reduce_end(0)
+    table[:, rank:] = identity
+    phase("elim1")
+    loop(0, 14, eliminate)
     phase("h_spread")
     reduce_spread(1)
-    phase("elim3")
-    loop(22, rank // group, eliminate)
+    phase("elim2")
+    loop(14, rank // group, eliminate)
     pivots = jnp.sum(table[:, :rank] * identity, axis=1, keepdims=True)
     inverse = table[:, rank:] / jnp.sqrt(pivots)
     row_basis = dot_split(row_image, inverse, NT)
 
     phase("drain")
-    for turn in range(4):
-        half_copy(turn).wait_send()
-    fwd_copy.wait_send()
+    for shift in range(4):
+        half_copy(shift).wait_send()
+    for lines in range(4):
+        fwd_copy(lines).wait_send()
     arrived(rs_send.at[pl.ds(0, PLANE - 1)], rs_ssem)
     arrived(image.at[pl.ds(0, PLANE - 1)], ag_ssem)
     arrived(z_in.at[pl.ds(0, DEPTH - 1)], z_ssem)
@@ -501,7 +548,8 @@
     def rows_wait_send(index):
         @pl.when(rows_target(index) != row)
         def _():
-            rows_copy(index).wait_send()
+            for part in range(PARTS):
+                rows_copy(part, index).wait_send()
 
     loop(0, DEPTH, rows_wait_send)
 
@@ -547,7 +595,7 @@
     vmem = pl.BlockSpec(memory_space=pltpu.VMEM)
     hbm = pl.BlockSpec(memory_space=pltpu.HBM)
     dma = pltpu.SemaphoreType.DMA
-    matrix = pltpu.VMEM((rows, cols), BF16)
+    matrix = pltpu.VMEM((8, rows, cols // 8), BF16)
     chunk = (CHUNK, rank)
     chunks = pltpu.VMEM((PLANE, *chunk), F32)
     pieces = pltpu.VMEM((2, PLANE, 8, rank), F32)
@@ -556,7 +604,7 @@
         out_shape=(
             jax.ShapeDtypeStruct((rows, 3 * rank), BF16),
             jax.ShapeDtypeStruct((cols, 3 * rank), BF16),
-            jax.ShapeDtypeStruct((rows, cols), BF16),
+            jax.ShapeDtypeStruct((8, rows, cols // 8), BF16),
         ),
         in_specs=[hbm, hbm, hbm, hbm],
         out_specs=(vmem, vmem, vmem),
@@ -570,7 +618,7 @@
             chunks,
             chunks,
             chunks,
-            chunks,
+            pltpu.VMEM((PARTS, PLANE, PART, rank), F32),
             pltpu.VMEM((2 * PLANE, *chunk), F32),
             pltpu.VMEM((DEPTH, *chunk), F32),
             pltpu.VMEM((8, *chunk), F32),
@@ -586,15 +634,15 @@
             dma((4,)),
             dma((4,)),
             dma,
+            dma((PARTS,)),
             dma,
+            dma((4,)),
+            dma((4,)),
+            dma((4,)),
             dma,
-            dma,
-            dma,
-            dma,
-            dma,
-            dma,
-            dma((8,)),
-            dma((8,)),
+            dma((PARTS, DEPTH)),
+            dma((PARTS, 8)),
+            dma((PARTS, 8)),
             dma((2,)),
             dma((2,)),
             dma((2,)),
@@ -610,9 +658,10 @@
 
 
 def finish_kernel(left, right, dual, estimate_hbm, dual_hbm, estimate_out, dual_out, out_sem):
-    rows, cols = dual.shape
+    rows, cols = estimate_out.shape
     width = rows
     row = lax.axis_index("row")
+    own_line = lax.div(row, 8)
     on_diagonal = lax.div(row, cols // rows) == lax.axis_index("col")
     row_ids = lax.broadcasted_iota(jnp.int32, (rows, width), 0)
     col_ids = lax.broadcasted_iota(jnp.int32, (rows, width), 1)
@@ -628,6 +677,10 @@
             ),
         )
 
+    def dual_block(index):
+        side = jnp.where(lax.div(index, 4) == lax.rem(row, 2), 1, 0)
+        return dual[4 * side + lax.rem(index + 4 - own_line, 4)]
+
     def tile(block):
         window = pl.ds(pl.multiple_of(block * width, width), width)
         theta = dot(left[...], right[pl.ds(pl.multiple_of(block * width, width), width), :], NT)
@@ -635,7 +688,8 @@
             on_diagonal & (block == lax.rem(row, cols // rows)), base_level, 0.0
         ).astype(F32)
         theta = theta + jnp.where(row_ids == col_ids, level, 0.0)
-        mixture = theta + dual[:, window].astype(F32)
+        kept = jnp.concatenate([dual_block(2 * block), dual_block(2 * block + 1)], axis=1)
+        mixture = theta + kept.astype(F32)
         clipped = jnp.clip(mixture, -threshold, threshold)
         estimate_out[:, window] = mixture - clipped
         dual_out[:, window] = clipped.astype(BF16)
@@ -648,8 +702,8 @@
             copy.wait()
 
 
-def finish(left, right, dual_var):
-    rows, cols = dual_var.shape
+def finish(left, right, dual_kept):
+    rows, cols = left.shape[0], right.shape[0]
     vmem = pl.BlockSpec(memory_space=pltpu.VMEM)
     hbm = pl.BlockSpec(memory_space=pltpu.HBM)
     return pl.pallas_call(
@@ -667,7 +721,7 @@
         ],
         compiler_params=pltpu.CompilerParams(vmem_limit_bytes=FINISH_VMEM),
         name="finish",
-    )(left, right, dual_var)
+    )(left, right, dual_kept)
 
 
 def body(covariance, estimate, dual_var, start_basis):

time: 61.7 us -> 57.5 us (0.932)
  Pallas kernels: 60 us -> 55.8 us
    pallas_call x1, Pallas kernels: 56.6 us -> 52.4 us  [solve(): pl.pallas_call(solve_kernel, out_shape=(jax.ShapeDtypeStruct((rows, 3 * r...]
where the time goes in v3:
time: 57.5 us; the launch traced here: 57.4 us
  Pallas kernels  55.8 us (97%)
  local copies, waits for them, and re-layouts  0.94 us (2%)
  between operations  0.65 us (1%)
    pallas_call x1, Pallas kernels, solve(): pl.pallas_call(solve_kernel, out_shape=(jax.ShapeDtypeStruct((rows, 3 * r...  52.4 us
    pallas_call x1, Pallas kernels, finish(): pl.pallas_call(finish_kernel, out_shape=(jax.ShapeDtypeStruct((rows, cols...  3.36 us

profile of v3, /device:TPU:1, one launch (start us, length us, event | category | flops | bytes accessed | tf_op | source)
XLA Modules:
  0.0 57.4 jit_solution(17084500230135700961)
XLA Ops:
  0.6 0.0 copy-start
  0.6 0.9 %copy-done = f32[512,128]{1,0:T(8,128)S(1)} copy-done((f32[512,128]{1,0:T(8,128)S(1)}, f32[512,128]{1,0:T(8,128)}, u32[]{:S(2)}) %copy-start) | copy-done | bytes 262168
  1.6 52.4 %solve.1 = (bf16[512,384]{1,0:T(8,128)(2,1)S(1)}, bf16[2048,384]{1,0:T(8,128)(2,1)S(1)}, bf16[8,512,256]{2,1,0:T(8,128)(2,1)S(1)}) custom-call(bf16[512,2048]{1,0:T(8,128)(2,1)} %cov_hbm.1, bf16[512,2048]{1,0:T(8,128)(2,1)} %est_hbm.1, bf16[512,2048]{1,0:T(8,128)(2,1)} %dual_hbm.1, f32[512,128]{1,0:T(8,128)S(1)} %copy-done), custom_call_target="tpu_custom_call" | custom-call | tf_op jit(solution)/shard_map/solve/pallas_call | solution.py:602
  54.0 3.4 %finish.1 = (f32[512,2048]{1,0:T(8,128)}, bf16[512,2048]{1,0:T(8,128)(2,1)}) custom-call(bf16[512,384]{1,0:T(8,128)(2,1)S(1)} %get-tuple-element.5.left, bf16[2048,384]{1,0:T(8,128)(2,1)S(1)} %get-tuple-element.6.right, bf16[8,512,256]{2,1,0:T(8,128)(2,1)S(1)} %get-tuple-element.7.dual), custom_call_target="tpu_custom_call" | custom-call | tf_op jit(solution)/shard_map/finish/pallas_call | solution.py:709
Async XLA Ops:
  0.6 1.0 %copy-start = (f32[512,128]{1,0:T(8,128)S(1)}, f32[512,128]{1,0:T(8,128)}, u32[]{:S(2)}) copy-start(f32[512,128]{1,0:T(8,128)} %basis_hbm.1) | copy-start | bytes 786436

commit v4 on v3

--- a/solution.py
+++ b/solution.py
@@ -134,11 +134,9 @@
     z_rsem,
     rows_ssem,
     rows_rsem,
-    a_ssem,
+    red_ssem,
     a_rsem,
-    b_ssem,
     b_rsem,
-    c_ssem,
     c_rsem,
 ):
     phase = Phase()
@@ -160,12 +158,12 @@
         offset = (1 - core if side == 0 else core) * half + lax.rem(own_line + shift, 4) * width
         window = pl.ds(pl.multiple_of(offset, width), width)
         return pltpu.make_async_copy(
-            source.at[:, window], target.at[4 * side + shift], load_sem.at[index, side, shift]
+            source.at[:, window], target.at[4 * side + shift], load_sem.at[shift]
         )
 
     basis_load = pltpu.make_async_copy(basis_hbm, basis, basis_sem)
     basis_load.start()
-    for shift in SHIFTS:
+    for shift in SHIFTS[:1]:
         for side in range(2):
             for index in range(3):
                 load(index, side, shift).start()
@@ -210,6 +208,11 @@
 
     has_own = lax.rem(row, 4) == lax.div(own_chunk, 8)
     peers = PLANE - 1 + 2 * DEPTH - 1 + 8 - jnp.where(has_own, 1, 0)
+
+    for shift in SHIFTS[1:]:
+        for side in range(2):
+            for index in range(3):
+                load(index, side, shift).start()
 
     phase("first")
     basis_load.wait()
@@ -218,9 +221,7 @@
     flip_both = jnp.concatenate([flip_high, flip_low], axis=0)
 
     def load_wait(shift):
-        for side in range(2):
-            for index in range(3):
-                load(index, side, shift).wait()
+        arrived(a_high.at[pl.ds(0, 6)], load_sem.at[shift])
 
     def partial_terms(shift):
         for side, target in ((0, part_other), (1, part_own)):
@@ -240,7 +241,7 @@
         return pltpu.make_async_remote_copy(
             src_ref=part_other.at[block],
             dst_ref=half_in.at[block],
-            send_sem=half_send.at[shift],
+            send_sem=half_send,
             recv_sem=half_recv.at[shift],
             device_id=(other, col),
             device_id_type=MESH,
@@ -294,7 +295,7 @@
             src_ref=image.at[own_chunk, part_rows[part]],
             dst_ref=z_in.at[col, part_rows[part]],
             send_sem=z_ssem,
-            recv_sem=z_rsem.at[part, d],
+            recv_sem=z_rsem.at[part],
             device_id=(row, lax.rem(col + d, DEPTH)),
             device_id_type=MESH,
         )
@@ -313,7 +314,7 @@
         return pltpu.make_async_remote_copy(
             src_ref=red_part.at[which, target],
             dst_ref=red_in.at[which, chip],
-            send_sem=a_ssem.at[which],
+            send_sem=red_ssem.at[which],
             recv_sem=a_rsem.at[which],
             device_id=(2 * target + core, col),
             device_id_type=MESH,
@@ -323,7 +324,7 @@
         return pltpu.make_async_remote_copy(
             src_ref=red_mid.at[which],
             dst_ref=red_mid_in.at[which, 2 * col + core],
-            send_sem=b_ssem.at[which],
+            send_sem=red_ssem.at[which],
             recv_sem=b_rsem.at[which],
             device_id=device,
             device_id_type=MESH,
@@ -333,7 +334,7 @@
         return pltpu.make_async_remote_copy(
             src_ref=red_out.at[which, chip],
             dst_ref=red_out.at[which, chip],
-            send_sem=c_ssem.at[which],
+            send_sem=red_ssem.at[which],
             recv_sem=c_rsem.at[which],
             device_id=(2 * target + core, col),
             device_id_type=MESH,
@@ -387,13 +388,14 @@
             ag_copy(part, target, offset[0]).start()
 
     slot = lax.rem(own_chunk, 8)
+    part_bytes = rs_in.at[0]
 
     def rows_copy(part, index):
         return pltpu.make_async_remote_copy(
             src_ref=z_in.at[index, part_rows[part]],
             dst_ref=rows_in.at[slot, part_rows[part]],
-            send_sem=rows_ssem.at[part, index],
-            recv_sem=rows_rsem.at[part, slot],
+            send_sem=rows_ssem,
+            recv_sem=rows_rsem,
             device_id=(rows_target(index), col),
             device_id_type=MESH,
         )
@@ -407,9 +409,10 @@
         def _():
             rows_in[slot, part_rows[part]] = z_in[index, part_rows[part]]
 
-    def forward(part, d):
-        arrived(z_in.at[0, part_rows[part]], z_rsem.at[part, d])
-        rows_start(part, lax.rem(col + DEPTH - d, DEPTH))
+    def forward(part):
+        arrived(part_bytes.at[pl.ds(0, DEPTH - 1)], z_rsem.at[part])
+        for d in DEPTH_OFFSETS:
+            rows_start(part, lax.rem(col + DEPTH - d, DEPTH))
 
     def fwd_copy(lines):
         line = lax.rem(own_line + 4 - lines, 4)
@@ -417,8 +420,8 @@
         return pltpu.make_async_remote_copy(
             src_ref=chunks,
             dst_ref=chunks,
-            send_sem=fwd_send.at[lines],
-            recv_sem=fwd_recv.at[lines],
+            send_sem=fwd_send,
+            recv_sem=fwd_recv,
             device_id=(other, col),
             device_id_type=MESH,
         )
@@ -455,32 +458,33 @@
     phase("z0")
     for part in range(PARTS):
         rows_start(part, col)
-    for d in DEPTH_OFFSETS:
-        forward(0, d)
+    for part in range(PARTS - 1):
+        forward(part)
     phase("g_mid")
     reduce_middle(0)
     phase("z1")
-    for d in DEPTH_OFFSETS:
-        forward(1, d)
+    forward(PARTS - 1)
     phase("lines")
     for lines in (2, 1, 3, 0):
         line_in(lines)
     phase("product0")
     product_terms(0)
     phase("fwd_wait")
-    for lines in range(4):
-        fwd_copy(lines).wait_recv()
+    arrived(part_other, fwd_recv)
     phase("product1")
     product_terms(1)
 
-    def rows_wait(index):
-        @pl.when(rows_source(index) != row)
+    def rows_done(sem):
+        @pl.when(has_own)
         def _():
-            for part in range(PARTS):
-                arrived(rows_in.at[index, part_rows[part]], rows_rsem.at[part, index])
+            arrived(rows_in.at[pl.ds(0, 7)], sem)
+
+        @pl.when(jnp.logical_not(has_own))
+        def _():
+            arrived(rows_in, sem)
 
     phase("rows_wait")
-    loop(0, 8, rows_wait)
+    rows_done(rows_rsem)
     phase("h_part")
     row_image = rows_in[...].reshape(8 * CHUNK, rank)
     reduce_start(1, dot_split(row_image, product[...], TN))
@@ -537,21 +541,13 @@
     row_basis = dot_split(row_image, inverse, NT)
 
     phase("drain")
-    for shift in range(4):
-        half_copy(shift).wait_send()
-    for lines in range(4):
-        fwd_copy(lines).wait_send()
+    arrived(part_other, half_send)
+    arrived(part_other, fwd_send)
     arrived(rs_send.at[pl.ds(0, PLANE - 1)], rs_ssem)
     arrived(image.at[pl.ds(0, PLANE - 1)], ag_ssem)
     arrived(z_in.at[pl.ds(0, DEPTH - 1)], z_ssem)
 
-    def rows_wait_send(index):
-        @pl.when(rows_target(index) != row)
-        def _():
-            for part in range(PARTS):
-                rows_copy(part, index).wait_send()
-
-    loop(0, DEPTH, rows_wait_send)
+    rows_done(rows_ssem)
 
     phase("h_end")
     inner = reduce_end(1)
@@ -583,9 +579,8 @@
     left_out[:, rank : 2 * rank] = weighted_high
     left_out[:, 2 * rank : 3 * rank] = weighted_low
     for which in range(2):
-        arrived(red_in.at[which, pl.ds(0, PLANE - 1)], a_ssem.at[which])
-        arrived(red_mid_in.at[which, pl.ds(0, 2 * DEPTH - 1)], b_ssem.at[which])
-        arrived(red_out.at[which, pl.ds(0, PLANE - 1)], c_ssem.at[which])
+        pieces = 2 * (PLANE - 1) + 2 * DEPTH - 1
+        arrived(product.at[pl.ds(0, 8 * pieces)], red_ssem.at[which])
     phase(None)
 
 
@@ -629,22 +624,20 @@
             pieces,
             pieces,
             pltpu.VMEM((rank, 2 * rank), F32),
-            dma((3, 2, 4)),
-            dma,
             dma((4,)),
+            dma,
+            dma,
             dma((4,)),
             dma,
             dma((PARTS,)),
             dma,
             dma((4,)),
-            dma((4,)),
-            dma((4,)),
-            dma,
-            dma((PARTS, DEPTH)),
-            dma((PARTS, 8)),
-            dma((PARTS, 8)),
-            dma((2,)),
-            dma((2,)),
+            dma,
+            dma,
+            dma,
+            dma((PARTS,)),
+            dma,
+            dma,
             dma((2,)),
             dma((2,)),
             dma((2,)),
@@ -667,7 +660,7 @@
     col_ids = lax.broadcasted_iota(jnp.int32, (rows, width), 1)
 
     def copies(block):
-        window = pl.ds(pl.multiple_of(block * width, width), width)
+        window = pl.ds(block * width, width)
         return (
             pltpu.make_async_copy(
                 estimate_out.at[:, window], estimate_hbm.at[:, window], out_sem.at[0, block]
@@ -678,12 +671,12 @@
         )
 
     def dual_block(index):
-        side = jnp.where(lax.div(index, 4) == lax.rem(row, 2), 1, 0)
+        side = jnp.where(index // 4 == lax.rem(row, 2), 1, 0)
         return dual[4 * side + lax.rem(index + 4 - own_line, 4)]
 
     def tile(block):
-        window = pl.ds(pl.multiple_of(block * width, width), width)
-        theta = dot(left[...], right[pl.ds(pl.multiple_of(block * width, width), width), :], NT)
+        window = pl.ds(block * width, width)
+        theta = dot(left[...], right[window, :], NT)
         level = jnp.where(
             on_diagonal & (block == lax.rem(row, cols // rows)), base_level, 0.0
         ).astype(F32)
@@ -696,7 +689,8 @@
         for copy in copies(block):
             copy.start()
 
-    loop(0, cols // width, tile)
+    for block in range(cols // width):
+        tile(block)
     for block in range(cols // width):
         for copy in copies(block):
             copy.wait()
@@ -725,6 +719,7 @@
 
 
 def body(covariance, estimate, dual_var, start_basis):
+    start_basis = pltpu.with_memory_space_constraint(start_basis, pltpu.HBM)
     left, right, dual_kept = solve(covariance, estimate, dual_var, start_basis)
     return finish(left, right, dual_kept)
 

time: 57.5 us -> 55.7 us (0.969)
  local copies, waits for them, and re-layouts: 0.94 us -> 0 us
  Pallas kernels: 55.8 us -> 54.9 us
    unnamed x2 -> x0, local copies, waits for them, and re-layouts: 0.94 us -> none
    pallas_call x1, Pallas kernels: 52.4 us -> 51.7 us  [solve(): pl.pallas_call(solve_kernel, out_shape=(jax.ShapeDtypeStruct((rows, 3 * r...]
where the time goes in v4:
time: 55.7 us; the launch traced here: 55.6 us
  Pallas kernels  54.9 us (99%)
  between operations  0.64 us (1%)
    pallas_call x1, Pallas kernels, solve(): pl.pallas_call(solve_kernel, out_shape=(jax.ShapeDtypeStruct((rows, 3 * r...  51.7 us
    pallas_call x1, Pallas kernels, finish(): pl.pallas_call(finish_kernel, out_shape=(jax.ShapeDtypeStruct((rows, cols...  3.27 us

profile of v4, /device:TPU:1, one launch (start us, length us, event | category | flops | bytes accessed | tf_op | source)
XLA Modules:
  0.0 55.6 jit_solution(4927451513046600321)
XLA Ops:
  0.6 51.7 %solve.1 = (bf16[512,384]{1,0:T(8,128)(2,1)S(1)}, bf16[2048,384]{1,0:T(8,128)(2,1)S(1)}, bf16[8,512,256]{2,1,0:T(8,128)(2,1)S(1)}) custom-call(bf16[512,2048]{1,0:T(8,128)(2,1)} %cov_hbm.1, bf16[512,2048]{1,0:T(8,128)(2,1)} %est_hbm.1, bf16[512,2048]{1,0:T(8,128)(2,1)} %dual_hbm.1, f32[512,128]{1,0:T(8,128)} %basis_hbm.1), custom_call_target="tpu_custom_call" | custom-call | tf_op jit(solution)/shard_map/solve/pallas_call | solution.py:597
  52.3 3.3 %finish.1 = (f32[512,2048]{1,0:T(8,128)}, bf16[512,2048]{1,0:T(8,128)(2,1)}) custom-call(bf16[512,384]{1,0:T(8,128)(2,1)S(1)} %get-tuple-element.5.left, bf16[2048,384]{1,0:T(8,128)(2,1)S(1)} %get-tuple-element.6.right, bf16[8,512,256]{2,1,0:T(8,128)(2,1)S(1)} %get-tuple-element.7.dual), custom_call_target="tpu_custom_call" | custom-call | tf_op jit(solution)/shard_map/finish/pallas_call | solution.py:703

commit v5 on v4

--- a/solution.py
+++ b/solution.py
@@ -232,24 +232,23 @@
             a_low[slot] = low
             both = dot(flip_both, high)
             terms = both[:rank] + (both[rank:] + dot(flip_high, low))
-            target[4 * shift : 4 * shift + 4] = terms.T.reshape(4, CHUNK, rank)
-
-    part_rows = [pl.ds(PART * part, PART) for part in range(PARTS)]
+            target[shift] = terms.T.reshape(PARTS, 4, PART, rank)
+
+    own_place = lax.rem(chip, 4)
 
     def half_copy(shift):
-        block = pl.ds(4 * shift, 4)
-        return pltpu.make_async_remote_copy(
-            src_ref=part_other.at[block],
-            dst_ref=half_in.at[block],
+        return pltpu.make_async_remote_copy(
+            src_ref=part_other.at[shift],
+            dst_ref=half_in.at[shift],
             send_sem=half_send,
             recv_sem=half_recv.at[shift],
             device_id=(other, col),
             device_id_type=MESH,
         )
 
-    def rs_copy(part, place, target):
-        return pltpu.make_async_remote_copy(
-            src_ref=rs_send.at[place, part_rows[part]],
+    def rs_copy(part, shift, place, target):
+        return pltpu.make_async_remote_copy(
+            src_ref=rs_send.at[shift, part, place],
             dst_ref=rs_in.at[part, chip],
             send_sem=rs_ssem,
             recv_sem=rs_rsem.at[part],
@@ -260,14 +259,13 @@
     def send_terms(part, shift):
         for turn in (2, 1, 3, 0):
             if shift or turn:
-                place = 4 * shift + lax.rem(lax.rem(chip, 4) + turn, 4)
-                target = 4 * lax.rem(own_line + shift, 4) + lax.rem(lax.rem(chip, 4) + turn, 4)
-                rs_copy(part, place, target).start()
+                place = lax.rem(own_place + turn, 4)
+                target = 4 * lax.rem(own_line + shift, 4) + place
+                rs_copy(part, shift, place, target).start()
 
     def combine(shift):
         half_copy(shift).wait_recv()
-        block = slice(4 * shift, 4 * shift + 4)
-        rs_send[block] = part_own[block] + half_in[block]
+        rs_send[shift] = part_own[shift] + half_in[shift]
         send_terms(0, shift)
 
     load_wait(SHIFTS[0])
@@ -289,11 +287,13 @@
     for part in range(1, PARTS):
         for shift in SHIFTS:
             send_terms(part, shift)
-    own_place = lax.rem(chip, 4)
+    def own_piece(part):
+        return image.at[core, own_line, part, own_place]
+
     def z_copy(part, d):
         return pltpu.make_async_remote_copy(
-            src_ref=image.at[own_chunk, part_rows[part]],
-            dst_ref=z_in.at[col, part_rows[part]],
+            src_ref=own_piece(part),
+            dst_ref=z_in.at[col, part],
             send_sem=z_ssem,
             recv_sem=z_rsem.at[part],
             device_id=(row, lax.rem(col + d, DEPTH)),
@@ -302,10 +302,10 @@
 
     def ag_copy(part, target, lines):
         return pltpu.make_async_remote_copy(
-            src_ref=image.at[own_chunk, part_rows[part]],
-            dst_ref=image.at[own_chunk, part_rows[part]],
+            src_ref=own_piece(part),
+            dst_ref=own_piece(part),
             send_sem=ag_ssem,
-            recv_sem=ag_rsem.at[lines],
+            recv_sem=ag_rsem.at[part, lines],
             device_id=(2 * target + core, col),
             device_id_type=MESH,
         )
@@ -369,31 +369,39 @@
         arrived(red_out.at[which, pl.ds(0, PLANE - 1)], c_rsem.at[which])
         return red_out[which].reshape(rank, rank)
 
+    sums = []
     for part in range(PARTS):
         phase(f"rs_wait{part}")
         arrived(rs_in.at[part, pl.ds(0, PLANE - 1)], rs_rsem.at[part])
         phase(f"spread{part}")
-        rs_in[part, chip] = rs_send[own_place, part_rows[part]]
+        rs_in[part, chip] = rs_send[0, part, own_place]
         terms = rs_in[part, 0]
         for d in range(1, PLANE):
             terms = terms + rs_in[part, d]
-        image[own_chunk, part_rows[part]] = terms
-        z_in[col, part_rows[part]] = terms
+        image[core, own_line, part, own_place] = terms
+        z_in[col, part] = terms
+        sums.append(terms)
         for d in DEPTH_OFFSETS:
             z_copy(part, d).start()
+        gathers = [
+            ag_copy(part, target, offset[0])
+            for offset, target in zip(PLANE_OFFSETS, plane_chips, strict=True)
+        ]
+        first = 4 if part == PARTS - 1 else PLANE
+        for copy in gathers[:first]:
+            copy.start()
         if part == PARTS - 1:
-            total = image[own_chunk]
+            total = jnp.concatenate(sums, axis=0)
             reduce_start(0, dot_full(total, total, TN))
-        for offset, target in zip(PLANE_OFFSETS, plane_chips, strict=True):
-            ag_copy(part, target, offset[0]).start()
-
-    slot = lax.rem(own_chunk, 8)
+        for copy in gathers[first:]:
+            copy.start()
+
     part_bytes = rs_in.at[0]
 
     def rows_copy(part, index):
         return pltpu.make_async_remote_copy(
-            src_ref=z_in.at[index, part_rows[part]],
-            dst_ref=rows_in.at[slot, part_rows[part]],
+            src_ref=z_in.at[index, part],
+            dst_ref=rows_in.at[lax.rem(own_line, 2), part, own_place],
             send_sem=rows_ssem,
             recv_sem=rows_rsem,
             device_id=(rows_target(index), col),
@@ -407,32 +415,33 @@
 
         @pl.when(rows_target(index) == row)
         def _():
-            rows_in[slot, part_rows[part]] = z_in[index, part_rows[part]]
+            rows_in[lax.rem(own_line, 2), part, own_place] = z_in[index, part]
 
     def forward(part):
         arrived(part_bytes.at[pl.ds(0, DEPTH - 1)], z_rsem.at[part])
         for d in DEPTH_OFFSETS:
             rows_start(part, lax.rem(col + DEPTH - d, DEPTH))
 
-    def fwd_copy(lines):
-        line = lax.rem(own_line + 4 - lines, 4)
-        chunks = image.at[pl.ds(core * PLANE + 4 * line, 4)]
-        return pltpu.make_async_remote_copy(
-            src_ref=chunks,
-            dst_ref=chunks,
+    def fwd_copy(part, lines):
+        pieces = image.at[core, lax.rem(own_line + 4 - lines, 4), part]
+        return pltpu.make_async_remote_copy(
+            src_ref=pieces,
+            dst_ref=pieces,
             send_sem=fwd_send,
-            recv_sem=fwd_recv,
+            recv_sem=fwd_recv.at[part],
             device_id=(other, col),
             device_id_type=MESH,
         )
 
-    def product_terms(side):
+    def product_terms(side, part, first=False):
         which = core if side == 0 else 1 - core
+        depth = width // PARTS
         highs, lows = [], []
         for shift in range(4):
-            block = which * PLANE + 4 * lax.rem(own_line + shift, 4)
-            window = pl.ds(pl.multiple_of(block * CHUNK, width), width)
-            high, low = split(image[pl.ds(block, 4)].reshape(width, rank))
+            line = lax.rem(own_line + shift, 4)
+            start = which * half + line * width + part * depth
+            window = pl.ds(pl.multiple_of(start, depth), depth)
+            high, low = split(image[which, line, part].reshape(depth, rank))
             right_out[window, 0:rank] = high
             right_out[window, rank : 2 * rank] = low
             right_out[window, 2 * rank : 3 * rank] = high
@@ -441,47 +450,59 @@
         right_high = jnp.concatenate(highs, axis=0)
         right_both = jnp.concatenate([right_high, jnp.concatenate(lows, axis=0)], axis=1)
         slots = range(4 * (1 - side), 4 * (1 - side) + 4)
+        inner = pl.ds(part * depth, depth)
+
+        def columns_of(matrix, rows):
+            return jnp.concatenate([matrix[slot, rows, inner] for slot in slots], axis=1)
+
         for start in range(0, product.shape[0], 256):
             rows = pl.ds(start, 256)
-            both = dot(jnp.concatenate([a_high[slot, rows] for slot in slots], axis=1), right_both)
-            terms = both[:, :rank] + (
-                both[:, rank:]
-                + dot(jnp.concatenate([a_low[slot, rows] for slot in slots], axis=1), right_high)
-            )
-            product[rows] = product[rows] + terms if side else terms
-
-    def line_in(lines):
+            both = dot(columns_of(a_high, rows), right_both)
+            terms = both[:, :rank] + (both[:, rank:] + dot(columns_of(a_low, rows), right_high))
+            product[rows] = terms if first else product[rows] + terms
+
+    def line_in(part, lines):
         count = 4 if lines else 3
-        arrived(image.at[pl.ds(0, count)], ag_rsem.at[lines])
-        fwd_copy(lines).start()
+        arrived(part_bytes.at[pl.ds(0, count)], ag_rsem.at[part, lines])
+        fwd_copy(part, lines).start()
+
+    def partner_in(part):
+        arrived(part_other.at[pl.ds(0, 4 // PARTS)], fwd_recv.at[part])
 
     phase("z0")
     for part in range(PARTS):
         rows_start(part, col)
-    for part in range(PARTS - 1):
-        forward(part)
+    forward(0)
+    phase("lines0")
+    for lines in (2, 1, 3, 0):
+        line_in(0, lines)
+    phase("product00")
+    product_terms(0, 0, True)
+    phase("z1")
+    forward(1)
+    phase("lines1")
+    for lines in (2, 1, 3, 0):
+        line_in(1, lines)
     phase("g_mid")
     reduce_middle(0)
-    phase("z1")
-    forward(PARTS - 1)
-    phase("lines")
-    for lines in (2, 1, 3, 0):
-        line_in(lines)
-    phase("product0")
-    product_terms(0)
+    phase("product10")
+    partner_in(0)
+    product_terms(1, 0)
+    phase("product01")
+    product_terms(0, 1)
     phase("fwd_wait")
-    arrived(part_other, fwd_recv)
+    partner_in(1)
     phase("product1")
-    product_terms(1)
+    product_terms(1, 1)
 
     def rows_done(sem):
         @pl.when(has_own)
         def _():
-            arrived(rows_in.at[pl.ds(0, 7)], sem)
+            arrived(part_bytes.at[pl.ds(0, 7 * PARTS)], sem)
 
         @pl.when(jnp.logical_not(has_own))
         def _():
-            arrived(rows_in, sem)
+            arrived(part_bytes, sem)
 
     phase("rows_wait")
     rows_done(rows_rsem)
@@ -499,10 +520,10 @@
             jnp.where(col_ids[: values.shape[0]] == lane, values, 0.0), axis=1, keepdims=True
         )
 
-    def eliminate(step):
+    def eliminate(step, low):
         first = step * group
         pivot_rows = [table[pl.ds(first + p, 1), :] for p in range(group)]
-        left_part = table[:, :rank]
+        left_part = table[low:, :rank]
         columns = [lane_of(left_part, first + p) for p in range(group)]
         entry = {
             (p, q): lane_of(pivot_rows[p][:, :rank], first + q)
@@ -512,7 +533,7 @@
         change = None
         for p in range(group):
             scale = 1.0 / entry[p, p]
-            factor = jnp.where(row_ids[:, :1] > first + p, columns[p] * scale, 0.0)
+            factor = jnp.where(row_ids[low:, :1] > first + p, columns[p] * scale, 0.0)
             for q in range(p + 1, group):
                 columns[q] = columns[q] - factor * entry[p, q]
                 weight = entry[p, q] * scale
@@ -521,7 +542,15 @@
                     entry[q, t] = entry[q, t] - weight * entry[p, t]
             term = factor * pivot_rows[p]
             change = term if change is None else change + term
-        table[...] = table[...] - change
+        table[low:, :] = table[low:, :] - change
+
+    def eliminate_part(number):
+        size = rank // 4
+        loop(
+            number * size // group,
+            (number + 1) * size // group,
+            functools.partial(eliminate, low=number * size),
+        )
 
     phase("g_spread")
     reduce_spread(0)
@@ -531,11 +560,13 @@
     table[:, :rank] = reduce_end(0)
     table[:, rank:] = identity
     phase("elim1")
-    loop(0, 14, eliminate)
+    eliminate_part(0)
+    eliminate_part(1)
     phase("h_spread")
     reduce_spread(1)
     phase("elim2")
-    loop(14, rank // group, eliminate)
+    eliminate_part(2)
+    eliminate_part(3)
     pivots = jnp.sum(table[:, :rank] * identity, axis=1, keepdims=True)
     inverse = table[:, rank:] / jnp.sqrt(pivots)
     row_basis = dot_split(row_image, inverse, NT)
@@ -543,9 +574,9 @@
     phase("drain")
     arrived(part_other, half_send)
     arrived(part_other, fwd_send)
-    arrived(rs_send.at[pl.ds(0, PLANE - 1)], rs_ssem)
-    arrived(image.at[pl.ds(0, PLANE - 1)], ag_ssem)
-    arrived(z_in.at[pl.ds(0, DEPTH - 1)], z_ssem)
+    arrived(rs_in.at[:, pl.ds(0, PLANE - 1)], rs_ssem)
+    arrived(rs_in.at[:, pl.ds(0, PLANE - 1)], ag_ssem)
+    arrived(rs_in.at[:, pl.ds(0, DEPTH - 1)], z_ssem)
 
     rows_done(rows_ssem)
 
@@ -591,8 +622,7 @@
     hbm = pl.BlockSpec(memory_space=pltpu.HBM)
     dma = pltpu.SemaphoreType.DMA
     matrix = pltpu.VMEM((8, rows, cols // 8), BF16)
-    chunk = (CHUNK, rank)
-    chunks = pltpu.VMEM((PLANE, *chunk), F32)
+    chunks = pltpu.VMEM((4, PARTS, 4, PART, rank), F32)
     pieces = pltpu.VMEM((2, PLANE, 8, rank), F32)
     return pl.pallas_call(
         solve_kernel,
@@ -614,9 +644,9 @@
             chunks,
             chunks,
             pltpu.VMEM((PARTS, PLANE, PART, rank), F32),
-            pltpu.VMEM((2 * PLANE, *chunk), F32),
-            pltpu.VMEM((DEPTH, *chunk), F32),
-            pltpu.VMEM((8, *chunk), F32),
+            pltpu.VMEM((2, 4, PARTS, 4, PART, rank), F32),
+            pltpu.VMEM((DEPTH, PARTS, PART, rank), F32),
+            pltpu.VMEM((2, PARTS, 4, PART, rank), F32),
             pltpu.VMEM((rows, rank), F32),
             pieces,
             pieces,
@@ -631,9 +661,9 @@
             dma,
             dma((PARTS,)),
             dma,
-            dma((4,)),
+            dma((PARTS, 4)),
             dma,
-            dma,
+            dma((PARTS,)),
             dma,
             dma((PARTS,)),
             dma,

time: 55.7 us -> 55.1 us (0.989)
  no operation moved by 1% of the time
where the time goes in v5:
time: 55.1 us; the launch traced here: 55 us
  Pallas kernels  54.4 us (99%)
  between operations  0.64 us (1%)
    pallas_call x1, Pallas kernels, solve(): pl.pallas_call(solve_kernel, out_shape=(jax.ShapeDtypeStruct((rows, 3 * r...  51.1 us
    pallas_call x1, Pallas kernels, finish(): pl.pallas_call(finish_kernel, out_shape=(jax.ShapeDtypeStruct((rows, cols...  3.26 us

profile of v5, /device:TPU:1, one launch (start us, length us, event | category | flops | bytes accessed | tf_op | source)
XLA Modules:
  0.0 55.0 jit_solution(14115216753917646799)
XLA Ops:
  0.6 51.1 %solve.1 = (bf16[512,384]{1,0:T(8,128)(2,1)S(1)}, bf16[2048,384]{1,0:T(8,128)(2,1)S(1)}, bf16[8,512,256]{2,1,0:T(8,128)(2,1)S(1)}) custom-call(bf16[512,2048]{1,0:T(8,128)(2,1)} %cov_hbm.1, bf16[512,2048]{1,0:T(8,128)(2,1)} %est_hbm.1, bf16[512,2048]{1,0:T(8,128)(2,1)} %dual_hbm.1, f32[512,128]{1,0:T(8,128)} %basis_hbm.1), custom_call_target="tpu_custom_call" | custom-call | tf_op jit(solution)/shard_map/solve/pallas_call | solution.py:627
  51.8 3.3 %finish.1 = (f32[512,2048]{1,0:T(8,128)}, bf16[512,2048]{1,0:T(8,128)(2,1)}) custom-call(bf16[512,384]{1,0:T(8,128)(2,1)S(1)} %get-tuple-element.5.left, bf16[2048,384]{1,0:T(8,128)(2,1)S(1)} %get-tuple-element.6.right, bf16[8,512,256]{2,1,0:T(8,128)(2,1)S(1)} %get-tuple-element.7.dual), custom_call_target="tpu_custom_call" | custom-call | tf_op jit(solution)/shard_map/finish/pallas_call | solution.py:733

commit v6 on v5

--- a/solution.py
+++ b/solution.py
@@ -37,6 +37,7 @@
     key=lambda o: -(ring(o[0], 4) + ring(o[1], 4)),
 )
 SHIFTS = (2, 1, 3, 0)
+FAR_PLANES = (3, 4, 5)
 DEPTH_OFFSETS = sorted(range(1, DEPTH), key=lambda d: -ring(d, DEPTH))
 COLUMN_OFFSETS = sorted(
     ((dz, dc) for dz in range(DEPTH) for dc in range(2) if dz or dc),
@@ -295,7 +296,7 @@
             src_ref=own_piece(part),
             dst_ref=z_in.at[col, part],
             send_sem=z_ssem,
-            recv_sem=z_rsem.at[part],
+            recv_sem=z_rsem.at[part, 0 if d in FAR_PLANES else 1],
             device_id=(row, lax.rem(col + d, DEPTH)),
             device_id_type=MESH,
         )
@@ -417,9 +418,10 @@
         def _():
             rows_in[lax.rem(own_line, 2), part, own_place] = z_in[index, part]
 
-    def forward(part):
-        arrived(part_bytes.at[pl.ds(0, DEPTH - 1)], z_rsem.at[part])
-        for d in DEPTH_OFFSETS:
+    def forward(part, far):
+        planes = [d for d in DEPTH_OFFSETS if (d in FAR_PLANES) == far]
+        arrived(part_bytes.at[pl.ds(0, len(planes))], z_rsem.at[part, 0 if far else 1])
+        for d in planes:
             rows_start(part, lax.rem(col + DEPTH - d, DEPTH))
 
     def fwd_copy(part, lines):
@@ -472,14 +474,17 @@
     phase("z0")
     for part in range(PARTS):
         rows_start(part, col)
-    forward(0)
+    forward(0, True)
+    forward(0, False)
     phase("lines0")
     for lines in (2, 1, 3, 0):
         line_in(0, lines)
     phase("product00")
     product_terms(0, 0, True)
     phase("z1")
-    forward(1)
+    forward(1, False)
+    phase("z1far")
+    forward(1, True)
     phase("lines1")
     for lines in (2, 1, 3, 0):
         line_in(1, lines)
@@ -665,7 +670,7 @@
             dma,
             dma((PARTS,)),
             dma,
-            dma((PARTS,)),
+            dma((PARTS, 2)),
             dma,
             dma,
             dma((2,)),
@@ -682,21 +687,22 @@
 
 def finish_kernel(left, right, dual, estimate_hbm, dual_hbm, estimate_out, dual_out, out_sem):
     rows, cols = estimate_out.shape
-    width = rows
+    narrow = cols // 8
+    blocks = [(0, narrow), (narrow, narrow)] + [
+        (start, 2 * narrow) for start in range(2 * narrow, cols, 2 * narrow)
+    ]
     row = lax.axis_index("row")
     own_line = lax.div(row, 8)
-    on_diagonal = lax.div(row, cols // rows) == lax.axis_index("col")
-    row_ids = lax.broadcasted_iota(jnp.int32, (rows, width), 0)
-    col_ids = lax.broadcasted_iota(jnp.int32, (rows, width), 1)
-
-    def copies(block):
-        window = pl.ds(block * width, width)
+    shift = row * rows - lax.axis_index("col") * cols
+
+    def copies(index):
+        window = pl.ds(*blocks[index])
         return (
             pltpu.make_async_copy(
-                estimate_out.at[:, window], estimate_hbm.at[:, window], out_sem.at[0, block]
+                estimate_out.at[:, window], estimate_hbm.at[:, window], out_sem.at[0, index]
             ),
             pltpu.make_async_copy(
-                dual_out.at[:, window], dual_hbm.at[:, window], out_sem.at[1, block]
+                dual_out.at[:, window], dual_hbm.at[:, window], out_sem.at[1, index]
             ),
         )
 
@@ -704,25 +710,26 @@
         side = jnp.where(index // 4 == lax.rem(row, 2), 1, 0)
         return dual[4 * side + lax.rem(index + 4 - own_line, 4)]
 
-    def tile(block):
-        window = pl.ds(block * width, width)
+    def tile(index):
+        start, width = blocks[index]
+        window = pl.ds(start, width)
         theta = dot(left[...], right[window, :], NT)
-        level = jnp.where(
-            on_diagonal & (block == lax.rem(row, cols // rows)), base_level, 0.0
-        ).astype(F32)
-        theta = theta + jnp.where(row_ids == col_ids, level, 0.0)
-        kept = jnp.concatenate([dual_block(2 * block), dual_block(2 * block + 1)], axis=1)
-        mixture = theta + kept.astype(F32)
+        offsets = lax.broadcasted_iota(jnp.int32, (rows, width), 1) - lax.broadcasted_iota(
+            jnp.int32, (rows, width), 0
+        )
+        theta = theta + jnp.where(offsets == shift - start, base_level, 0.0).astype(F32)
+        kept = [dual_block(n) for n in range(start // narrow, (start + width) // narrow)]
+        mixture = theta + jnp.concatenate(kept, axis=1).astype(F32)
         clipped = jnp.clip(mixture, -threshold, threshold)
         estimate_out[:, window] = mixture - clipped
         dual_out[:, window] = clipped.astype(BF16)
-        for copy in copies(block):
+        for copy in copies(index):
             copy.start()
 
-    for block in range(cols // width):
-        tile(block)
-    for block in range(cols // width):
-        for copy in copies(block):
+    for index in range(len(blocks)):
+        tile(index)
+    for index in range(len(blocks)):
+        for copy in copies(index):
             copy.wait()
 
 
@@ -741,7 +748,7 @@
         scratch_shapes=[
             pltpu.VMEM((rows, cols), F32),
             pltpu.VMEM((rows, cols), BF16),
-            pltpu.SemaphoreType.DMA((2, cols // rows)),
+            pltpu.SemaphoreType.DMA((2, 5)),
         ],
         compiler_params=pltpu.CompilerParams(vmem_limit_bytes=FINISH_VMEM),
         name="finish",

time: 55.1 us -> 55 us (level)
  no operation moved by 1% of the time
where the time goes in v6:
time: 55 us; the launch traced here: 54.9 us
  Pallas kernels  54.3 us (99%)
  between operations  0.64 us (1%)
    pallas_call x1, Pallas kernels, solve(): pl.pallas_call(solve_kernel, out_shape=(jax.ShapeDtypeStruct((rows, 3 * r...  50.9 us
    pallas_call x1, Pallas kernels, finish(): pl.pallas_call(finish_kernel, out_shape=(jax.ShapeDtypeStruct((rows, cols...  3.37 us

profile of v6, /device:TPU:1, one launch (start us, length us, event | category | flops | bytes accessed | tf_op | source)
XLA Modules:
  0.0 54.9 jit_solution(4949325112899850385)
XLA Ops:
  0.6 50.9 %solve.1 = (bf16[512,384]{1,0:T(8,128)(2,1)S(1)}, bf16[2048,384]{1,0:T(8,128)(2,1)S(1)}, bf16[8,512,256]{2,1,0:T(8,128)(2,1)S(1)}) custom-call(bf16[512,2048]{1,0:T(8,128)(2,1)} %cov_hbm.1, bf16[512,2048]{1,0:T(8,128)(2,1)} %est_hbm.1, bf16[512,2048]{1,0:T(8,128)(2,1)} %dual_hbm.1, f32[512,128]{1,0:T(8,128)} %basis_hbm.1), custom_call_target="tpu_custom_call" | custom-call | tf_op jit(solution)/shard_map/solve/pallas_call | solution.py:632
  51.5 3.4 %finish.1 = (f32[512,2048]{1,0:T(8,128)}, bf16[512,2048]{1,0:T(8,128)(2,1)}) custom-call(bf16[512,384]{1,0:T(8,128)(2,1)S(1)} %get-tuple-element.5.left, bf16[2048,384]{1,0:T(8,128)(2,1)S(1)} %get-tuple-element.6.right, bf16[8,512,256]{2,1,0:T(8,128)(2,1)S(1)} %get-tuple-element.7.dual), custom_call_target="tpu_custom_call" | custom-call | tf_op jit(solution)/shard_map/finish/pallas_call | solution.py:740
